TPU v7x, 8 devices: a whole 2x2x1 slice. The times are simulated.
8 devices in a mesh: dp: 8 (over z, y, x, core).
Axes of the slice: x: 2, y: 2, z: 1, core: 2. Of those that a mesh axis runs over, the one named last changes fastest.
Arguments:
- grad_wq: bfloat16 [8, 2, 1152, 1152], P('dp')
- grad_wk: bfloat16 [8, 2, 1152, 384], P('dp')
- grad_wv: bfloat16 [8, 2, 1152, 384], P('dp')
- grad_wo: bfloat16 [8, 2, 1152, 1152], P('dp')
- grad_gate: bfloat16 [8, 2, 1152, 3072], P('dp')
- grad_up: bfloat16 [8, 2, 1152, 3072], P('dp')
- grad_down: bfloat16 [8, 2, 3072, 1152], P('dp')
- grad_attn_norm: bfloat16 [8, 2, 1152], P('dp')
- grad_mlp_norm: bfloat16 [8, 2, 1152], P('dp')
- grad_final_norm: bfloat16 [8, 1152], P('dp')
- master: float32 [28317696], P('dp')
- exp_avg: float32 [28317696], P('dp')
- exp_avg_sq: float32 [28317696], P('dp')
- learn_rate: float32 [], replicated
Outputs:
- output 1: float32 [28317696], P('dp')
- output 2: float32 [28317696], P('dp')
- output 3: float32 [28317696], P('dp')
- output 4: bfloat16 [2, 1152, 1152], replicated
- output 5: bfloat16 [2, 1152, 384], replicated
- output 6: bfloat16 [2, 1152, 384], replicated
- output 7: bfloat16 [2, 1152, 1152], replicated
- output 8: bfloat16 [2, 1152, 3072], replicated
- output 9: bfloat16 [2, 1152, 3072], replicated
- output 10: bfloat16 [2, 3072, 1152], replicated
- output 11: bfloat16 [2, 1152], replicated
- output 12: bfloat16 [2, 1152], replicated
- output 13: bfloat16 [1152], replicated
- output 14: float32 [], replicated
All inputs are finite; a program needn't handle non-finite values.
Results may differ from a plain program's by a relative error of at most 0.001.
Values sent between devices are 32-bit elements.
A program may use at most 1 GiB of HBM per device.

v0:
```python
import math
import jax
import jax.numpy as jnp
from jax import lax
from jax.sharding import PartitionSpec as P

BETA_ONE = 0.9
BETA_TWO = 0.95
ADAM_EPS = 1e-8
WEIGHT_DECAY = 0.1
MAX_NORM = 1.0
CLIP_EPS = 1e-6
STEP = 4
BIAS_ONE = 1.0 - BETA_ONE ** STEP
BIAS_TWO = 1.0 - BETA_TWO ** STEP


def split_flat(flat_vec, shapes):
    tensors = []
    offset = 0
    for piece_shape in shapes:
        piece_size = math.prod(piece_shape)
        tensors.append(flat_vec[offset:offset + piece_size].reshape(piece_shape))
        offset += piece_size
    return tensors


def adam_update(grad_part, grad_norm, master, exp_avg, exp_avg_sq, learn_rate, decay_mask):
    clip_coef = jnp.minimum(1.0, MAX_NORM / (grad_norm + CLIP_EPS))
    clipped = clip_coef * grad_part
    new_avg = BETA_ONE * exp_avg + (1.0 - BETA_ONE) * clipped
    new_avg_sq = BETA_TWO * exp_avg_sq + (1.0 - BETA_TWO) * clipped * clipped
    adam_dir = (new_avg / BIAS_ONE) / (jnp.sqrt(new_avg_sq / BIAS_TWO) + ADAM_EPS)
    decay_term = jnp.where(decay_mask, WEIGHT_DECAY * master, 0.0)
    new_master = master - learn_rate * (decay_term + adam_dir)
    return new_master, new_avg, new_avg_sq


def solution(mesh):
    num_devices = mesh.shape["dp"]

    def optimizer_step(*arrays):
        shapes = [grad_array.shape[1:] for grad_array in arrays[:10]]
        counts = [math.prod(piece_shape) for piece_shape in shapes]
        total_count = sum(counts)
        matrix_count = sum(counts[:7])
        padded = arrays[10].shape[0]
        shard_len = padded // num_devices

        def local_step(*local_arrays):
            local_grads = local_arrays[:10]
            master, exp_avg, exp_avg_sq, learn_rate = local_arrays[10:]
            pieces = [local_grad.reshape(-1).astype(jnp.float32) for local_grad in local_grads]
            pieces.append(jnp.zeros((padded - total_count,), jnp.float32))
            local_flat = jnp.concatenate(pieces)
            grad_shard = lax.psum_scatter(local_flat, "dp", scatter_dimension=0, tiled=True) / num_devices
            grad_norm = jnp.sqrt(lax.psum(jnp.sum(grad_shard * grad_shard), "dp"))
            shard_start = lax.axis_index("dp") * shard_len
            decay_mask = (shard_start + jnp.arange(shard_len)) < matrix_count
            new_master, new_avg, new_avg_sq = adam_update(grad_shard, grad_norm, master, exp_avg, exp_avg_sq, learn_rate, decay_mask)
            full_master = lax.all_gather(new_master, "dp", tiled=True)
            params = split_flat(full_master[:total_count].astype(jnp.bfloat16), shapes)
            return tuple([new_master, new_avg, new_avg_sq] + params + [grad_norm])

        mapped = jax.shard_map(local_step, mesh=mesh, in_specs=(P("dp"),) * 13 + (P(),), out_specs=(P("dp"),) * 3 + (P(),) * 11, check_vma=False)
        return mapped(*arrays)

    return optimizer_step
```

profile of v0, /device:TPU:0, one launch (start us, length us, event | category | flops | bytes accessed | tf_op | source)
XLA Modules:
  0.0 2252.0 jit_solution(13871777239123581399)
XLA Ops:
  7.2 11.1 reshape.95
  18.3 9.2 constant_dynamic-update-slice_fusion.10
  27.5 2.5 reshape.96
  30.0 2.6 reshape.97
  32.6 11.1 reshape.98
  43.7 7.8 convert_element_type.91
  51.5 11.5 copy.28
  62.9 7.8 convert_element_type.92
  70.7 11.4 copy.29
  82.1 27.8 %reshape.101 = f32[7077888]{0:T(1024)} reshape(bf16[1,2,3072,1152]{3,2,1,0:T(8,128)(2,1)} %param.20) | data formatting | bytes 42467328 | tf_op jit(solution)/shard_map/convert_element_type | solution.py:53
  110.0 0.6 reshape.102
  110.6 0.7 reshape.103
  111.3 0.7 convert_reduce_fusion
  112.0 4.1 constant_dynamic-update-slice_fusion.9
  116.1 2.0 constant_dynamic-update-slice_fusion.8
  118.1 9.0 constant_dynamic-update-slice_fusion.7
  127.2 23.4 %constant_dynamic-update-slice_fusion.6 = f32[28317696]{0:T(1024)} fusion(f32[28317696]{0:T(1024)} %constant_dynamic-update-slice_fusion.7, f32[7077888]{0:T(1024)} %bitcast.15), kind=kLoop, calls=%fused_computation.14 | loop fusion | bytes 56623104
  150.6 1.9 slice-done.4
  152.5 1.2 slice-done.5
  153.7 0.9 slice-done.6
  154.6 9.5 constant_dynamic-update-slice_fusion.5
  164.2 19.7 constant_dynamic-update-slice_fusion.4
  183.9 1.3 constant_dynamic-update-slice_fusion.3
  185.2 1.3 constant_dynamic-update-slice_fusion.2
  186.5 1.3 constant_dynamic-update-slice_fusion.1
  187.9 1.3 constant_dynamic-update-slice_fusion
  189.2 0.0 all-gather.3.cloned.1.call-start
  189.9 1247.5 %all-reduce.3.cloned.1.call-done = f32[28317696]{0:T(1024)} async-done(((f32[28317696]{0:T(1024)}), f32[28317696]{0:T(1024)}) %all-reduce.3.cloned.1.call-update) | async-done | bytes 113270800
  1437.3 7.9 multiply_reduce_fusion
  1445.2 23.2 %psum.7 = f32[]{:T(128)} all-reduce(f32[]{:T(128)} %multiply_reduce_fusion), channel_id=1, replica_groups=mesh['dp'=8] {'dp'}, use_global_device_ids=true, to_apply=%region_2.0 | all-reduce | flops 1 | bytes 8 | tf_op jit(solution)/shard_map/psum | solution.py:57
  1469.2 33.1 %multiply_subtract_fusion = (f32[3539712]{0:T(1024)}, f32[3539712]{0:T(1024)}, f32[3539712]{0:T(1024)}) fusion(f32[3539712]{0:T(1024)} %param.24, s32[]{:T(128)S(6)} %mul.48, f32[]{:T(128)S(6)} %copy.41, f32[]{:T(128)S(6)} %mul.53, f32[28317696]{0:T(1024)} %all-reduce.3.cloned.1.call-done, u32[]{:T(128)S(6)} %multiply.6, f32[3539712]{0:T(1024)} %param.25, ...), kind=kLoop, calls=%fused_computation.3 | loop fusion | flops 67254528 | bytes 99111952 | tf_op jit(solution)/shard_map/sub | solution.py:35
  1502.3 54.1 %reshape.105 = f32[1,1,3539712]{2,1,0:T(1,128)} reshape(f32[3539712]{0:T(1024)} %get-tuple-element.14) | data formatting | bytes 28317696
  1556.4 494.7 %all-gather.3.cloned.1.call-done = f32[8,1,3539712]{2,1,0:T(1,128)} async-done(((f32[1,1,3539712]{2,1,0:T(1,128)}), f32[8,1,3539712]{2,1,0:T(1,128)}) %all-gather.3.cloned.1.call-update) | async-done | bytes 113270800 | tf_op jit(solution)/shard_map/all_gather | solution.py:61
  2051.1 53.8 %slice.66 = bf16[28317312]{0:T(1024)(128)(2,1)} slice(f32[28317696]{0:T(1024)} %bitcast), slice={[0:28317312]} | slice | bytes 113269248 | tf_op jit(solution)/shard_map/slice | solution.py:62
  2104.8 28.8 %fusion.3 = (bf16[7077888]{0:T(1024)(128)(2,1)}, bf16[7077888]{0:T(1024)(128)(2,1)}, bf16[7077888]{0:T(1024)(128)(2,1)}) fusion(bf16[28317312]{0:T(1024)(128)(2,1)} %slice.66), kind=kLoop, calls=%fused_computation.20 | loop fusion | bytes 84934656 | tf_op jit(solution)/shard_map/slice | solution.py:23
  2133.7 9.0 fusion.4
  2142.6 2.2 fusion.5
  2144.9 0.8 fusion.2
  2145.6 1.3 slice.64
  2146.9 21.6 reshape.92
  2168.5 21.6 reshape.93
  2190.0 26.9 %reshape.94 = bf16[2,3072,1152]{2,1,0:T(8,128)(2,1)} reshape(bf16[7077888]{0:T(1024)(128)(2,1)} %get-tuple-element.19) | data formatting | bytes 28311552 | tf_op jit(solution)/shard_map/reshape | solution.py:23
  2216.9 10.8 reshape.88
  2227.7 10.8 reshape.91
  2238.5 2.2 reshape.89
  2240.6 2.2 reshape.90
  2242.8 0.6 slice.50
  2243.4 0.6 slice.52
  (21 shorter events, 0.1 us)
Async XLA Ops:
  7.2 1430.1 %all-reduce.3.cloned.1.call-start = ((), (), s32[]{:S(2)}) async-start(), calls=%async_computation.1 | async-start | bytes 226541568
  18.3 9.2 copy-start
  82.1 27.8 %copy-start.2 = (bf16[1,2,1152]{2,1,0:T(2,128)(2,1)S(1)}, bf16[1,2,1152]{2,1,0:T(2,128)(2,1)}, u32[]{:S(2)}) copy-start(bf16[1,2,1152]{2,1,0:T(2,128)(2,1)} %param.21) | copy-start | bytes 13828
  127.1 23.5 %slice-start = ((s8[28311552]{0:T(1024)(128)(4,1)}), s8[4194304]{0:T(1024)(128)(4,1)S(1)}, s32[]{:S(2)}) async-start(s8[28311552]{0:T(1024)(128)(4,1)} %bitcast.16), calls=%async_computation.2 | async-start | bytes 8388608
  127.1 23.5 %slice-start.1 = ((s8[28311552]{0:T(1024)(128)(4,1)}), s8[4194304]{0:T(1024)(128)(4,1)S(1)}, s32[]{:S(2)}) async-start(s8[28311552]{0:T(1024)(128)(4,1)} %bitcast.16), calls=%async_computation.3 | async-start | bytes 8388608
  127.1 23.5 %slice-start.2 = ((s8[28311552]{0:T(1024)(128)(4,1)}), s8[4194304]{0:T(1024)(128)(4,1)S(1)}, s32[]{:S(2)}) async-start(s8[28311552]{0:T(1024)(128)(4,1)} %bitcast.16), calls=%async_computation.4 | async-start | bytes 8388608
  127.1 23.5 %slice-start.3 = ((s8[28311552]{0:T(1024)(128)(4,1)}), s8[4194304]{0:T(1024)(128)(4,1)S(1)}, s32[]{:S(2)}) async-start(s8[28311552]{0:T(1024)(128)(4,1)} %bitcast.16), calls=%async_computation.5 | async-start | bytes 8388608
  127.2 25.4 %slice-start.4 = ((s8[28311552]{0:T(1024)(128)(4,1)}), s8[4194304]{0:T(1024)(128)(4,1)S(1)}, s32[]{:S(2)}) async-start(s8[28311552]{0:T(1024)(128)(4,1)} %bitcast.16), calls=%async_computation.6 | async-start | bytes 8388608
  127.2 26.5 %slice-start.5 = ((s8[28311552]{0:T(1024)(128)(4,1)}), s8[4194304]{0:T(1024)(128)(4,1)S(1)}, s32[]{:S(2)}) async-start(s8[28311552]{0:T(1024)(128)(4,1)} %bitcast.16), calls=%async_computation.7 | async-start | bytes 8388608
  127.2 27.4 %slice-start.6 = ((s8[28311552]{0:T(1024)(128)(4,1)}), s8[3145728]{0:T(1024)(128)(4,1)S(1)}, s32[]{:S(2)}) async-start(s8[28311552]{0:T(1024)(128)(4,1)} %bitcast.16), calls=%async_computation.8 | async-start | bytes 6291456
  164.1 19.8 copy-start.1
  189.2 1861.9 %all-gather.3.cloned.1.call-start = ((), (), s32[]{:S(2)}) async-start(), calls=%async_computation | async-start | bytes 127429632 | tf_op jit(solution)/shard_map/all_gather | solution.py:61
Sparse Core Ops, SparseCore 0:
  189.3 1248.0 all-reduce.2
  1556.5 494.5 all-gather.2
where the time goes:
time: 2260 us; the launch traced here: 2250 us
  waiting for transfers between devices  1740 us (77%)
  local copies, waits for them, and re-layouts  413 us (18%)
  other arithmetic  57.3 us (3%)
  blocking collectives  23.2 us (1%)
    unnamed x3, waiting for transfers between devices  1250 us
    all_gather x1, waiting for transfers between devices, local_step(): full_master = lax.all_gather(new_master, 'dp', tiled=True)  495 us
    unnamed x33, local copies, waits for them, and re-layouts  162 us
    reshape x7, local copies, waits for them, and re-layouts, split_flat(): tensors.append(flat_vec[offset:offset + piece_size].reshape(piece_shape))  95.9 us
    convert_element_type x7, local copies, waits for them, and re-layouts, local_step(): local_grad.reshape(-1).astype(jnp.float32)  56.5 us
    slice x1, local copies, waits for them, and re-layouts, local_step(): params = split_flat(full_master[:total_count].astype(jnp.bfloat16), shapes)  53.8 us
  transfers between devices with their start and end apart: 2, of which 2 were waited for; matrix products, arithmetic and copies ran while one was open for 0% of the time, Pallas kernels for 0%

commit v1 on v0

v1 whole, which is shorter than its diff:
```python
import functools
import jax
import jax.numpy as jnp
from jax import lax
from jax.experimental import pallas as pl
from jax.experimental.pallas import tpu as pltpu
from jax.sharding import PartitionSpec as P

BETA_ONE = 0.9
BETA_TWO = 0.95
ADAM_EPS = 1e-8
WEIGHT_DECAY = 0.1
MAX_NORM = 1.0
CLIP_EPS = 1e-6
STEP = 4
BIAS_ONE = 1.0 - BETA_ONE ** STEP
BIAS_TWO = 1.0 - BETA_TWO ** STEP

MESH = pl.DeviceIdType.MESH
LANES = 128
SEG_TILES = 3456
SEG_ROWS = SEG_TILES * 8
LOCAL_ROWS = SEG_ROWS + 6
MATRIX_ROWS = 8 * SEG_ROWS
TAIL = 48
N = 216
ROWS = N * 8
HALF = 8
RING = 4
LAG = 5
WIDTHS = (24, 9, 3)


def neighbours(me):
    core = lax.rem(me, 2)
    x = lax.rem(lax.div(me, 2), 2)
    y = lax.div(me, 4)
    flip = 1 - 2 * core
    xn = me + 2 - 4 * x
    yn = me + 4 - 8 * y
    diag = xn + 4 - 8 * y
    return flip, me + flip, xn, yn, diag


def on_piece(refs, seg, tile, act):
    wq, wk, wv, wo, gate, up, down = refs
    pl.when((seg == 0) & (tile < 2592))(lambda: act(wq, tile))
    pl.when((seg == 0) & (tile >= 2592))(lambda: act(wk, tile - 2592))
    pl.when((seg == 1) & (tile < 864))(lambda: act(wv, tile))
    pl.when((seg == 1) & (tile >= 864))(lambda: act(wo, tile - 864))
    pl.when((seg == 2) | (seg == 3))(lambda: act(gate, (seg - 2) * SEG_TILES + tile))
    pl.when((seg == 4) | (seg == 5))(lambda: act(up, (seg - 4) * SEG_TILES + tile))
    pl.when((seg == 6) | (seg == 7))(lambda: act(down, (seg - 6) * SEG_TILES + tile))


def on_width(seg, tile, act):
    narrow = ((seg == 0) & (tile >= 2592)) | ((seg == 1) & (tile < 864))
    wide = (seg >= 2) & (seg < 6)
    pl.when(wide)(lambda: act(24))
    pl.when(narrow)(lambda: act(3))
    pl.when(jnp.logical_not(wide | narrow))(lambda: act(9))


def load_piece(refs, seg, tile, buf, sem):
    def act(ref, off):
        pltpu.make_async_copy(ref.at[pl.ds(off, N)], buf, sem).start()
    on_piece(refs, seg, tile, act)


def store_piece(refs, seg, tile, buf, sem):
    def act(ref, off):
        pltpu.make_async_copy(buf, ref.at[pl.ds(off, N)], sem).start()
    on_piece(refs, seg, tile, act)


def tiles_loop(body, group=12):
    def step(i, carry):
        body(pl.ds(pl.multiple_of(i * group, group), group))
        return carry
    lax.fori_loop(0, N // group, step, 0)


def remote(src, dst, send, recv, dev):
    return pltpu.make_async_remote_copy(src_ref=src, dst_ref=dst, send_sem=send, recv_sem=recv, device_id=(dev,), device_id_type=MESH)


def greet(devs):
    barrier = pltpu.get_barrier_semaphore()
    for dev in devs:
        pl.semaphore_signal(barrier, inc=1, device_id=(dev,), device_id_type=MESH)
    pl.semaphore_wait(barrier, len(devs))


def reduce_kernel(wq, wk, wv, wo, gate, up, down, gtail, g_out, n_out, land_x, land_y, land_p,
                  raw_p, raw_q, raw_o, got, fwd, stage_p, stage, own_in, own_g, norm_send, norm_land,
                  s_x, s_y, s_p, r_x, r_y, r_p, l_p, l_q, l_o, l_got, l_fwd, l_own, l_g, l_t, s_n, r_n):
    refs = (wq, wk, wv, wo, gate, up, down)
    me = lax.axis_index("dp")
    flip, partner, xn, yn, diag = neighbours(me)
    greet((partner, xn, yn))
    tail_copy = pltpu.make_async_copy(gtail, g_out.at[pl.ds(SEG_ROWS, TAIL)], l_t)
    tail_copy.start()
    n_out[...] = jnp.zeros_like(n_out)

    def job(s, link):
        j = lax.rem(s, HALF)
        first = jnp.where(s < 16, link, 1 - link)
        seg = jnp.where(s < 8, diag, xn if link == 0 else yn)
        return seg, first * (HALF * N) + j * N

    def give(jobs, par, wait_old):
        for a, (seg, tile, slot) in enumerate(jobs):
            load_piece(refs, seg + flip, tile, raw_p.at[a], l_p.at[a])
        for a, (seg, tile, slot) in enumerate(jobs):
            pltpu.make_async_copy(wq.at[pl.ds(0, N)], raw_p.at[a], l_p.at[a]).wait()
            copy = remote(stage_p.at[par, a], land_p.at[slot], s_p.at[par, a], r_p.at[slot], partner)
            pl.when(wait_old)(copy.wait_send)

            def conv(d, a=a):
                stage_p[par, a, d] = raw_p[a, d].astype(jnp.float32)
            tiles_loop(conv)
            copy.start()

    def link_jobs(s):
        return [job(s, link) + (link * 24 + s,) for link in (0, 1)]

    def own_jobs(j):
        return [(me, h * HALF * N + j * N, 48 + h * HALF + j) for h in (0, 1)]

    def fetch(src, buf, sem):
        pltpu.make_async_copy(src, buf, sem).start()

    def fetched(src, buf, sem):
        pltpu.make_async_copy(src, buf, sem).wait()

    give(link_jobs(0), 0, False)

    def step(s, count):
        j = lax.rem(s, HALF)
        more = s < 23
        own_give = (s >= 23) & (s < 31)

        @pl.when(more)
        def _():
            par = lax.rem(s + 1, 2)
            give(link_jobs(s + 1), par, s >= 1)

        @pl.when(s < 24)
        def _():
            ring = lax.rem(s, RING)
            jobs = link_jobs(s)
            for a, (seg, tile, slot) in enumerate(jobs):
                load_piece(refs, seg, tile, raw_q.at[a], l_q.at[a])
            for a, (seg, tile, slot) in enumerate(jobs):
                remote(stage_p.at[0, a], land_p.at[slot], s_p.at[0, a], r_p.at[slot], partner).wait_recv()
                fetch(land_p.at[slot], got.at[a], l_got.at[a])

            @pl.when(s >= 16)
            def _():
                remote(stage.at[0, 0], land_x.at[j], s_x.at[0], r_x.at[j], xn).wait_recv()
                remote(stage.at[0, 1], land_y.at[j], s_y.at[0], r_y.at[j], yn).wait_recv()
                fetch(land_y.at[j], fwd.at[0], l_fwd.at[0])
                fetch(land_x.at[j], fwd.at[1], l_fwd.at[1])
            copies = [remote(stage.at[ring, 0], land_x.at[s], s_x.at[ring], r_x.at[s], xn),
                      remote(stage.at[ring, 1], land_y.at[s], s_y.at[ring], r_y.at[s], yn)]
            for a in (0, 1):
                fetched(wq.at[pl.ds(0, N)], raw_q.at[a], l_q.at[a])
                fetched(land_p.at[0], got.at[a], l_got.at[a])
                pl.when(s >= RING)(copies[a].wait_send)

                @pl.when(s < 16)
                def _(a=a):
                    def add(d):
                        stage[ring, a, d] = raw_q[a, d].astype(jnp.float32) + got[a, d]
                    tiles_loop(add)

                @pl.when(s >= 16)
                def _(a=a):
                    fetched(land_x.at[0], fwd.at[a], l_fwd.at[a])

                    def add(d):
                        stage[ring, a, d] = raw_q[a, d].astype(jnp.float32) + got[a, d] + fwd[a, d]
                    tiles_loop(add)
                copies[a].start()

        @pl.when((s >= 12) & (s < 20))
        def _():
            give_own(s - 12)

        @pl.when(s >= 16 + LAG)
        def _():
            take_own(s - 16 - LAG)
        return count

    def give_own(j):
        for h, (seg, tile, slot) in enumerate(own_jobs(j)):
            load_piece(refs, seg + flip, tile, raw_o.at[h], l_o.at[h])
        for h, (seg, tile, slot) in enumerate(own_jobs(j)):
            fetched(wq.at[pl.ds(0, N)], raw_o.at[h], l_o.at[h])
            copy = remote(stage_p.at[2, h], land_p.at[slot], s_p.at[2, h], r_p.at[slot], partner)
            pl.when(j >= 1)(copy.wait_send)

            def conv(d, h=h):
                stage_p[2, h, d] = raw_o[h, d].astype(jnp.float32)
            tiles_loop(conv)
            copy.start()

    def take_own(j):
        for h, (seg, tile, slot) in enumerate(own_jobs(j)):
            load_piece(refs, seg, tile, raw_o.at[h], l_o.at[h])
            remote(stage_p.at[2, h], land_p.at[slot], s_p.at[2, h], r_p.at[slot], partner).wait_recv()
            fetch(land_p.at[slot], own_in.at[h, 0], l_own.at[h, 0])
        for h in (0, 1):
            one, two = 8 + j, 16 + j
            if h == 0:
                remote(stage.at[0, 0], land_x.at[one], s_x.at[0], r_x.at[one], xn).wait_recv()
                fetch(land_x.at[one], own_in.at[h, 1], l_own.at[h, 1])
            else:
                remote(stage.at[0, 1], land_y.at[one], s_y.at[0], r_y.at[one], yn).wait_recv()
                fetch(land_y.at[one], own_in.at[h, 1], l_own.at[h, 1])
        for h in (0, 1):
            if h == 0:
                remote(stage.at[0, 1], land_y.at[two], s_y.at[0], r_y.at[two], yn).wait_recv()
                fetch(land_y.at[two], own_in.at[h, 2], l_own.at[h, 2])
            else:
                remote(stage.at[0, 0], land_x.at[two], s_x.at[0], r_x.at[two], xn).wait_recv()
                fetch(land_x.at[two], own_in.at[h, 2], l_own.at[h, 2])
        for h, (seg, tile, slot) in enumerate(own_jobs(j)):
            fetched(wq.at[pl.ds(0, N)], raw_o.at[h], l_o.at[h])
            for a in range(3):
                fetched(land_p.at[0], own_in.at[h, a], l_own.at[h, a])
            row = pl.multiple_of(tile * 8, 8)
            out = pltpu.make_async_copy(own_g.at[h], g_out.at[pl.ds(row, ROWS)], l_g.at[h])
            pl.when(j >= 1)(out.wait)

            def relay(width, h=h):
                def body(r, acc):
                    for w in range(width):
                        t = r * width + w
                        g = (raw_o[h, t].astype(jnp.float32) + own_in[h, 0, t] + own_in[h, 1, t] + own_in[h, 2, t]) * 0.125
                        own_g[h, pl.ds(r * (8 * width) + w, 8, stride=width), :] = g
                        acc = acc + g * g
                    return acc
                n_out[...] += lax.fori_loop(0, N // width, body, jnp.zeros((8, LANES), jnp.float32))
            on_width(me, tile, relay)
            out.start()

    lax.fori_loop(0, 24 + LAG, step, 0)

    for r, dev in enumerate((partner, xn, yn)):
        norm_send[r] = n_out[...]
        copy = remote(norm_send.at[r], norm_land.at[r], s_n.at[r], r_n.at[r], dev)
        copy.start()
        copy.wait()
        n_out[...] += norm_land[r]
    tail_copy.wait()
    for a in (0, 1):
        for par in range(3):
            remote(stage_p.at[par, a], land_p.at[0], s_p.at[par, a], r_p.at[0], partner).wait_send()
        pltpu.make_async_copy(own_g.at[a], g_out.at[pl.ds(0, ROWS)], l_g.at[a]).wait()
    for ring in range(RING):
        remote(stage.at[ring, 0], land_x.at[0], s_x.at[ring], r_x.at[0], xn).wait_send()
        remote(stage.at[ring, 1], land_y.at[0], s_y.at[ring], r_y.at[0], yn).wait_send()


def gather_kernel(g_in, p_in, m_in, v_in, head, scal, p_out, m_out, v_out, wq, wk, wv, wo, gate, up, down, land,
                  gb, st, pb, stage, cin, cout, s_x, s_y, s_p, r_x, r_y, r_o, r_px, r_py, f_x, f_y, d_x, d_y,
                  l_in, l_out, l_c, l_o):
    refs = (wq, wk, wv, wo, gate, up, down)
    me = lax.axis_index("dp")
    flip, partner, xn, yn, diag = neighbours(me)
    greet((partner, xn, yn))
    coef, lr = scal[0], scal[1]
    shift = 6 * me
    pb[pl.ds(0, TAIL), :] = head[...]
    ins, outs = (p_in, m_in, v_in), (p_out, m_out, v_out)

    def at(seg, c):
        return land.at[seg, pl.ds(pl.multiple_of(c * N, N), N)]

    def link_piece(q, link):
        seg = jnp.where(q < 16, xn if link == 0 else yn, diag)
        chunk = jnp.where(q < 16, q, q - 8 if link == 0 else q - 16)
        return seg, chunk

    def own(s):
        ring = lax.rem(s, RING)
        row = pl.multiple_of(s * ROWS, 8)
        pltpu.make_async_copy(g_in.at[pl.ds(row, ROWS + TAIL)], gb, l_in.at[3]).start()
        for a in range(3):
            @pl.when(s >= 1)
            def _(a=a):
                pltpu.make_async_copy(st.at[a], outs[a].at[pl.ds(row, ROWS)], l_out.at[a]).wait()
            pltpu.make_async_copy(ins[a].at[pl.ds(row, ROWS)], st.at[a], l_in.at[a]).start()
        pltpu.make_async_copy(g_in.at[pl.ds(row, ROWS + TAIL)], gb, l_in.at[3]).wait()
        for a in range(3):
            pltpu.make_async_copy(ins[a].at[pl.ds(row, ROWS)], st.at[a], l_in.at[a]).wait()
        slab = 48
        base = me * LOCAL_ROWS + s * ROWS

        def update(i, carry):
            d = pl.ds(pl.multiple_of(i * slab, 8), slab)
            e = pl.ds(i * slab + shift, slab)
            g = gb[e, :] * coef
            p = st[0, d, :]
            m = BETA_ONE * st[1, d, :] + (1.0 - BETA_ONE) * g
            v = BETA_TWO * st[2, d, :] + (1.0 - BETA_TWO) * g * g
            direction = (m * (1.0 / BIAS_ONE)) / (jnp.sqrt(v * (1.0 / BIAS_TWO)) + ADAM_EPS)
            place = lax.broadcasted_iota(jnp.int32, (slab, LANES), 0) + (base + i * slab)
            decay = jnp.where(place < MATRIX_ROWS, WEIGHT_DECAY * p, 0.0)
            p = p - lr * (decay + direction)
            st[0, d, :] = p
            st[1, d, :] = m
            st[2, d, :] = v
            pb[e, :] = p
            return carry
        lax.fori_loop(0, ROWS // slab, update, 0)
        for a in range(3):
            pltpu.make_async_copy(st.at[a], outs[a].at[pl.ds(row, ROWS)], l_out.at[a]).start()
        copies = [remote(stage.at[ring], at(me, s), s_x.at[ring], r_x.at[s], xn),
                  remote(stage.at[ring], at(me, s), s_y.at[ring], r_y.at[s], yn),
                  remote(stage.at[ring], at(me, s), s_p.at[ring], r_o.at[s], partner)]

        @pl.when(s >= RING)
        def _():
            for copy in copies:
                copy.wait_send()

        def relay(width):
            def body(r, carry):
                for w in range(width):
                    t = r * width + w
                    stage[ring, t] = pb[pl.ds(r * (8 * width) + w, 8, stride=width), :]
                return carry
            lax.fori_loop(0, N // width, body, 0)
        on_width(me, s * N, relay)
        pb[pl.ds(0, TAIL), :] = pb[pl.ds(ROWS, TAIL), :]
        for copy in copies:
            copy.start()

        def conv(d):
            cout[0, d] = stage[ring, d].astype(jnp.bfloat16)
        tiles_loop(conv)
        store_piece(refs, me, s * N, cout.at[0], l_o.at[0])

    def convert(slot, seg, chunk):
        pltpu.make_async_copy(at(0, 0), cin.at[slot - 1], l_c.at[slot - 1]).wait()

        def conv(d):
            cout[slot, d] = cin[slot - 1, d].astype(jnp.bfloat16)
        tiles_loop(conv)
        store_piece(refs, seg, chunk * N, cout.at[slot], l_o.at[slot])

    def fetch(slot, seg, chunk):
        pltpu.make_async_copy(at(seg, chunk), cin.at[slot - 1], l_c.at[slot - 1]).start()

    def stored(slot):
        pltpu.make_async_copy(cout.at[slot], wq.at[pl.ds(0, N)], l_o.at[slot]).wait()

    def step(s, carry):
        j = s - 16
        q = s - LAG
        q2 = s - LAG - 1

        @pl.when((s >= 1) & (s <= 16))
        def _():
            stored(0)

        @pl.when(s < 16)
        def _():
            own(s)

        @pl.when((s >= 16) & (s < 24))
        def _():
            remote(at(xn, j), at(xn, j), f_y.at[j], r_y.at[s], yn).start()
            remote(at(yn, 8 + j), at(yn, 8 + j), f_x.at[j], r_x.at[s], xn).start()

        @pl.when((q >= 1) & (q <= 24))
        def _():
            stored(1)
            stored(2)

        @pl.when((q2 >= 1) & (q2 <= 24))
        def _():
            stored(3)
            stored(4)

        @pl.when((q2 >= 1) & (q2 <= 16))
        def _():
            stored(5)

        xseg, xc = link_piece(q, 0)
        yseg, yc = link_piece(q, 1)
        par = lax.rem(s, 2)

        @pl.when((q >= 0) & (q < 24))
        def _():
            remote(at(xseg, xc), at(xseg, xc), d_x.at[par], r_x.at[q], xn).wait_recv()
            copy = remote(at(xseg, xc), at(xseg, xc), d_x.at[par], r_px.at[q], partner)
            pl.when(q >= 2)(copy.wait_send)
            copy.start()
            fetch(1, xseg, xc)
            remote(at(yseg, yc), at(yseg, yc), d_y.at[par], r_y.at[q], yn).wait_recv()
            copy = remote(at(yseg, yc), at(yseg, yc), d_y.at[par], r_py.at[q], partner)
            pl.when(q >= 2)(copy.wait_send)
            copy.start()
            fetch(2, yseg, yc)

        pxseg, pxc = link_piece(q2, 0)
        pyseg, pyc = link_piece(q2, 1)

        @pl.when((q2 >= 0) & (q2 < 16))
        def _():
            remote(at(partner, q2), at(partner, q2), s_p.at[0], r_o.at[q2], partner).wait_recv()
            fetch(5, partner, q2)

        @pl.when((q2 >= 0) & (q2 < 24))
        def _():
            remote(at(0, 0), at(0, 0), d_x.at[par], r_px.at[q2], partner).wait_recv()
            fetch(3, pxseg + flip, pxc)
            remote(at(0, 0), at(0, 0), d_y.at[par], r_py.at[q2], partner).wait_recv()
            fetch(4, pyseg + flip, pyc)

        @pl.when((q >= 0) & (q < 24))
        def _():
            convert(1, xseg, xc)
            convert(2, yseg, yc)

        @pl.when((q2 >= 0) & (q2 < 16))
        def _():
            convert(5, partner, q2)

        @pl.when((q2 >= 0) & (q2 < 24))
        def _():
            convert(3, pxseg + flip, pxc)
            convert(4, pyseg + flip, pyc)
        return carry

    lax.fori_loop(0, 24 + LAG + 1, step, 0)
    stored(3)
    stored(4)
    for a in range(3):
        pltpu.make_async_copy(st.at[a], outs[a].at[pl.ds(0, ROWS)], l_out.at[a]).wait()
    for ring in range(RING):
        remote(stage.at[ring], at(me, 0), s_x.at[ring], r_x.at[0], xn).wait_send()
        remote(stage.at[ring], at(me, 0), s_y.at[ring], r_y.at[0], yn).wait_send()
        remote(stage.at[ring], at(me, 0), s_p.at[ring], r_o.at[0], partner).wait_send()
    for j in range(HALF):
        remote(at(0, 0), at(0, 0), f_y.at[j], r_y.at[0], yn).wait_send()
        remote(at(0, 0), at(0, 0), f_x.at[j], r_x.at[0], xn).wait_send()
    for par in (0, 1):
        remote(at(0, 0), at(0, 0), d_x.at[par], r_px.at[0], partner).wait_send()
        remote(at(0, 0), at(0, 0), d_y.at[par], r_py.at[0], partner).wait_send()


ANY = pl.BlockSpec(memory_space=pl.ANY)
VMEM = pl.BlockSpec(memory_space=pltpu.VMEM)
SMEM = pl.BlockSpec(memory_space=pltpu.SMEM)
F32 = jnp.float32
BF16 = jnp.bfloat16
LIMIT = 62 * 1024 * 1024


def to_tiles(x):
    rows, cols = x.shape[-2:]
    lead = x.size // cols
    return x.reshape(lead // 8, 8, cols // LANES, LANES).transpose(0, 2, 1, 3).reshape(-1, 8, LANES)


def from_tiles(t, shape):
    cols = shape[-1]
    lead = t.size // cols
    return t.reshape(lead // 8, cols // LANES, 8, LANES).transpose(0, 2, 1, 3).reshape(shape)


def reduce_call(tiles, gtail):
    dma = pltpu.SemaphoreType.DMA
    chunk = (N, 8, LANES)
    return pl.pallas_call(
        reduce_kernel,
        out_shape=[jax.ShapeDtypeStruct((SEG_ROWS + TAIL, LANES), F32), jax.ShapeDtypeStruct((8, LANES), F32),
                   jax.ShapeDtypeStruct((24,) + chunk, F32), jax.ShapeDtypeStruct((24,) + chunk, F32),
                   jax.ShapeDtypeStruct((64,) + chunk, F32)],
        in_specs=[ANY] * 7 + [VMEM],
        out_specs=[ANY, VMEM, ANY, ANY, ANY],
        scratch_shapes=[pltpu.VMEM((2,) + chunk, BF16), pltpu.VMEM((2,) + chunk, BF16), pltpu.VMEM((2,) + chunk, BF16),
                        pltpu.VMEM((2,) + chunk, F32), pltpu.VMEM((2,) + chunk, F32), pltpu.VMEM((3, 2) + chunk, F32),
                        pltpu.VMEM((RING, 2) + chunk, F32), pltpu.VMEM((2, 3) + chunk, F32), pltpu.VMEM((2, ROWS, LANES), F32),
                        pltpu.VMEM((3, 8, LANES), F32), pltpu.VMEM((3, 8, LANES), F32),
                        dma((RING,)), dma((RING,)), dma((3, 2)), dma((24,)), dma((24,)), dma((64,)),
                        dma((2,)), dma((2,)), dma((2,)), dma((2,)), dma((2,)), dma((2, 3)), dma((2,)), dma, dma((3,)), dma((3,))],
        compiler_params=pltpu.CompilerParams(collective_id=0, has_side_effects=True, vmem_limit_bytes=LIMIT),
        name="reduce_grads",
    )(*tiles, gtail)


def gather_call(g, p, m, v, head, scal):
    dma = pltpu.SemaphoreType.DMA
    chunk = (N, 8, LANES)
    flat = jax.ShapeDtypeStruct((LOCAL_ROWS, LANES), F32)
    tile_counts = (2592, 864, 864, 2592, 6912, 6912, 6912)
    return pl.pallas_call(
        gather_kernel,
        out_shape=[flat] * 3 + [jax.ShapeDtypeStruct((c, 8, LANES), BF16) for c in tile_counts]
        + [jax.ShapeDtypeStruct((8, SEG_TILES, 8, LANES), F32)],
        in_specs=[ANY] * 4 + [VMEM, SMEM],
        out_specs=[ANY] * 11,
        scratch_shapes=[pltpu.VMEM((ROWS + TAIL, LANES), F32), pltpu.VMEM((3, ROWS, LANES), F32), pltpu.VMEM((ROWS + TAIL, LANES), F32),
                        pltpu.VMEM((RING,) + chunk, F32), pltpu.VMEM((5,) + chunk, F32), pltpu.VMEM((6,) + chunk, BF16),
                        dma((RING,)), dma((RING,)), dma((RING,)), dma((24,)), dma((24,)), dma((16,)), dma((24,)), dma((24,)),
                        dma((HALF,)), dma((HALF,)), dma((2,)), dma((2,)), dma((4,)), dma((3,)), dma((5,)), dma((6,))],
        compiler_params=pltpu.CompilerParams(collective_id=1, has_side_effects=True, vmem_limit_bytes=LIMIT),
        name="update_gather",
    )(g, p, m, v, head, scal)


def adam(g, p, m, v, lr, decay):
    m = BETA_ONE * m + (1.0 - BETA_ONE) * g
    v = BETA_TWO * v + (1.0 - BETA_TWO) * g * g
    direction = (m / BIAS_ONE) / (jnp.sqrt(v / BIAS_TWO) + ADAM_EPS)
    return p - lr * (decay * p + direction), m, v


def local_step(*arrays):
    grads = arrays[:10]
    master, exp_avg, exp_avg_sq, lr = arrays[10:]
    me = lax.axis_index("dp")
    wq, wk, wv, wo, gate, up, down = grads[:7]
    width = TAIL * LANES
    gains = jnp.concatenate([g.reshape(-1) for g in grads[7:]] + [jnp.zeros((width - 5760,), BF16)])
    firsts = [wv[0, 0, :16], gate[0, 0, :2], gate[0, 1, :2], up[0, 0, :2], up[0, 1, :2], down[0, 0, :6], down[0, 1, :6]]
    heads = jnp.stack([f.reshape(-1)[:width] for f in firsts] + [gains]).astype(F32) * 0.125
    gt = lax.psum(heads, "dp").reshape(8, TAIL, LANES)
    window = jnp.stack([a[-width:] for a in (master, exp_avg, exp_avg_sq)])
    window = jnp.pad(window, ((0, 0), (0, width)))
    window = lax.dynamic_slice(window, (0, (42 - 6 * me) * LANES), (3, width))
    tails = lax.all_gather(window, "dp").reshape(8, 3, TAIL, LANES)
    gtail = lax.dynamic_index_in_dim(gt, me, 0, keepdims=False)

    g, squares = reduce_call([to_tiles(x) for x in grads[:7]], gtail)[:2]
    norm = jnp.sqrt(jnp.sum(squares) + jnp.sum(gt[7] * gt[7]))
    coef = jnp.minimum(1.0, MAX_NORM / (norm + CLIP_EPS))
    decay = jnp.where(lax.broadcasted_iota(jnp.int32, (8, TAIL, LANES), 0) < 7, WEIGHT_DECAY, 0.0)
    new_tails = adam(coef * gt, tails[:, 0], tails[:, 1], tails[:, 2], lr, decay)
    head = lax.dynamic_index_in_dim(new_tails[0], lax.rem(me + 7, 8), 0, keepdims=False)
    res = gather_call(g, *[a.reshape(LOCAL_ROWS, LANES) for a in (master, exp_avg, exp_avg_sq)], head, jnp.stack([coef, lr]))
    states = []
    for full, tail in zip(res[:3], new_tails):
        last = lax.dynamic_slice(tail, (me, 6 * me, 0), (1, 6, LANES))[0]
        states.append(lax.dynamic_update_slice(full, last, (SEG_ROWS, 0)).reshape(-1))
    params = [from_tiles(t, x.shape[1:]) for t, x in zip(res[3:10], grads[:7])]
    gains = new_tails[0][7].reshape(-1).astype(BF16)
    params += [gains[:2304].reshape(2, 1152), gains[2304:4608].reshape(2, 1152), gains[4608:5760]]
    return tuple(states + params + [norm])


def solution(mesh):
    return jax.shard_map(local_step, mesh=mesh, in_specs=(P("dp"),) * 13 + (P(),), out_specs=(P("dp"),) * 3 + (P(),) * 11, check_vma=False)
```

time: 2260 us -> 1090 us (0.48)
  waiting for transfers between devices: 1740 us -> 25.7 us
  Pallas kernels: 0 us -> 943 us
  local copies, waits for them, and re-layouts: 413 us -> 80.6 us
  other arithmetic: 57.3 us -> 4.34 us
    unnamed x3 -> x1, waiting for transfers between devices: 1250 us -> 0.02 us
    pallas_call x0 -> x2, Pallas kernels: none -> 943 us  [the longest x1 474 us: reduce_call(): pl.pallas_call(reduce_kernel, out_shape=[jax.ShapeDtypeStruct((SEG_ROWS +...]
    all_gather x1 -> x0, waiting for transfers between devices: 495 us -> none  [local_step(): full_master = lax.all_gather(new_master, 'dp', tiled=True)]
    slice x8, local copies, waits for them, and re-layouts: 97.1 us -> 3.62 us  [the longest x3 2.26 us: local_step(): window = jnp.stack([a[-width:] for a in (master, exp_avg, exp_avg_sq)])]
    reshape x7 -> x5, local copies, waits for them, and re-layouts: 95.9 us -> 3.04 us  [the longest x2 1.41 us: local_step(): g.reshape(-1)]
    unnamed x33 -> x59, local copies, waits for them, and re-layouts: 162 us -> 71.1 us
    convert_element_type x7 -> x0, local copies, waits for them, and re-layouts: 56.5 us -> none  [local_step(): local_grad.reshape(-1).astype(jnp.float32)]
    sub x1 -> x0, other arithmetic: 33.1 us -> none  [adam_update(): new_master = master - learn_rate * (decay_term + adam_dir)]
  transfers between devices with their start and end apart: 2 -> 1, of which waited for: 2 -> 1; matrix products, arithmetic and copies ran while one was open for 0% -> 0% of each run, Pallas kernels for 0% -> 0%
where the time goes in v1:
time: 1090 us
  Pallas kernels  943 us (87%)
  local copies, waits for them, and re-layouts  80.6 us (7%)
  waiting for transfers between devices  25.7 us (2%)
  between operations  17.5 us (2%)
  blocking collectives  16.3 us (1%)
    pallas_call x1, Pallas kernels, reduce_call(): pl.pallas_call(reduce_kernel, out_shape=[jax.ShapeDtypeStruct((SEG_ROWS +...  474 us
    pallas_call x1, Pallas kernels, gather_call(): pl.pallas_call(gather_kernel, out_shape=[flat] * 3 + [jax.ShapeDtypeStruc...  469 us
    unnamed x59, local copies, waits for them, and re-layouts  71.1 us
    psum x1, waiting for transfers between devices, local_step(): gt = lax.psum(heads, 'dp').reshape(8, TAIL, LANES)  25.7 us
  transfers between devices with their start and end apart: 1, of which 1 were waited for; matrix products, arithmetic and copies ran while one was open for 0% of the time, Pallas kernels for 0%

profile of v1, /device:TPU:0, one launch (start us, length us, event | category | flops | bytes accessed | tf_op | source)
XLA Modules:
  0.0 1087.1 jit_solution(2779660706391824773)
XLA Ops:
  7.2 0.0 all-reduce.3.cloned.1.call-start
  7.2 0.7 reshape.177
  7.9 0.7 reshape.178
  8.6 0.7 reduce.1
  9.4 0.7 slice_bitcast_fusion.7
  10.1 0.8 slice_bitcast_fusion.5
  11.0 0.8 slice_bitcast_fusion.3
  11.9 0.7 fusion.16
  12.9 0.3 stack.36
  13.1 0.7 convert_multiply_fusion
  13.8 0.0 all-reduce.3.cloned.1.call-update
  14.5 0.8 slice.78
  15.3 0.8 slice.79
  16.0 0.8 slice.80
  16.8 0.2 fusion.9
  17.0 16.3 %all-gather.1 = f32[8,3,6144]{2,1,0:T(4,128)S(1)} all-gather(f32[1,3,6144]{2,1,0:T(4,128)S(1)} %fusion.9), channel_id=2, replica_groups=mesh['dp'=8] {'dp'}, dimensions={0}, use_global_device_ids=true | all-gather | bytes 663552 | tf_op jit(solution)/shard_map/all_gather | solution.py:537
  33.2 0.4 reshape.209
  33.7 25.7 %all-reduce.3.cloned.1.call-done = f32[8,6144]{1,0:T(8,128)} async-done(((f32[8,6144]{1,0:T(8,128)}), f32[8,6144]{1,0:T(8,128)}) %all-reduce.3.cloned.1.call-update) | async-done | bytes 196624 | tf_op jit(solution)/shard_map/psum | solution.py:533
  59.4 1.0 copy.49
  60.3 0.6 dynamic-slice_bitcast_fusion.1.gtail
  61.0 474.0 %reduce_grads.1 = (f32[27696,128]{1,0:T(8,128)}, f32[8,128]{1,0:T(8,128)}, f32[24,216,8,128]{3,2,1,0:T(8,128)}, f32[24,216,8,128]{3,2,1,0:T(8,128)}, f32[64,216,8,128]{3,2,1,0:T(8,128)}) custom-call(bf16[2592,8,128]{2,1,0:T(8,128)(2,1)} %bitcast.183, bf16[864,8,128]{2,1,0:T(8,128)(2,1)} %bitcast.188, bf16[864,8,128]{2,1,0:T(8,128)(2,1)} %bitcast.185, ...), custom_call_target="tpu_custom_call" | custom-call | tf_op jit(solution)/shard_map/reduce_grads/pallas_call | solution.py:479
  535.0 1.3 reduce_sum.18
  536.3 0.7 fusion.12
  538.3 0.2 fusion.13
  538.5 0.6 slice_bitcast_fusion.8
  539.1 0.6 reshape.203
  539.7 0.6 reshape.202
  540.4 0.6 pad_maximum_fusion.1.scal
  540.9 0.6 dynamic-slice_bitcast_fusion.head
  541.5 468.6 %update_gather.1 = (f32[27654,128]{1,0:T(8,128)}, f32[27654,128]{1,0:T(8,128)}, f32[27654,128]{1,0:T(8,128)}, bf16[2592,8,128]{2,1,0:T(8,128)(2,1)}, bf16[864,8,...) custom-call(f32[27696,128]{1,0:T(8,128)} %get-tuple-element.26.g_in,, ...), custom_call_target="tpu_custom_call" | custom-call | tf_op jit(solution)/shard_map/update_gather/pallas_call | solution.py:502
  1010.2 0.6 bitcast_dynamic-update-slice_fusion.2
  1010.8 0.6 bitcast_dynamic-update-slice_fusion
  1011.4 11.8 %copy.65 = f32[3539712]{0:T(1024)} copy(f32[3539712]{0:T(1024)} %bitcast.171) | data formatting | bytes 28317696
  1023.2 2.5 copy-done
  1025.6 7.2 copy.66
  1032.8 1.5 slice-done.2
  1034.3 0.4 slice-done.3
  1034.8 7.2 copy.67
  1042.0 6.0 copy.68
  1048.0 1.2 copy.69
  1049.2 1.2 copy.70
  1050.5 5.4 copy.71
  1056.0 7.2 copy.72
  1063.1 1.4 slice-done.11
  1064.5 7.2 copy.73
  1071.7 1.7 slice-done.6
  1073.4 0.4 slice-done.7
  1073.8 5.3 copy.74
  (54 shorter events, 0.3 us)
Async XLA Ops:
  7.2 52.2 %all-reduce.3.cloned.1.call-start = ((), (), s32[]{:S(2)}) async-start(), calls=%async_computation | async-start | bytes 393216 | tf_op jit(solution)/shard_map/psum | solution.py:533
  61.0 475.3 %copy-start.3 = (f32[8,6144]{1,0:T(8,128)S(1)}, f32[8,6144]{1,0:T(8,128)}, u32[]{:S(2)}) copy-start(f32[8,6144]{1,0:T(8,128)} %all-reduce.3.cloned.1.call-done) | copy-start | bytes 589828
  1011.4 14.2 %copy-start = (f32[27654,128]{1,0:T(8,128)S(1)}, f32[27654,128]{1,0:T(8,128)}, u32[]{:S(2)}) copy-start(f32[27654,128]{1,0:T(8,128)} %get-tuple-element.51) | copy-start | bytes 42476548
  1011.4 21.4 %slice-start = ((s8[14159872]{0:T(1024)(128)(4,1)}), s8[4194304]{0:T(1024)(128)(4,1)S(1)}, s32[]{:S(2)}) async-start(s8[14159872]{0:T(1024)(128)(4,1)} %bitcast.168), calls=%async_computation.1 | async-start | bytes 8388608
  1011.4 21.4 %slice-start.1 = ((s8[14159872]{0:T(1024)(128)(4,1)}), s8[4194304]{0:T(1024)(128)(4,1)S(1)}, s32[]{:S(2)}) async-start(s8[14159872]{0:T(1024)(128)(4,1)} %bitcast.168), calls=%async_computation.2 | async-start | bytes 8388608
  1025.6 8.7 slice-start.2
  1025.6 9.1 slice-start.3
  1034.8 13.3 %copy-start.2 = (bf16[864,8,128]{2,1,0:T(8,128)(2,1)S(1)}, bf16[864,8,128]{2,1,0:T(8,128)(2,1)}, u32[]{:S(2)}) copy-start(bf16[864,8,128]{2,1,0:T(8,128)(2,1)} %get-tuple-element.32) | copy-start | bytes 5308420
  1034.8 21.1 %slice-start.12 = ((s8[14155776]{0:T(1024)(128)(4,1)}), s8[1572864]{0:T(1024)(128)(4,1)S(1)}, s32[]{:S(2)}) async-start(s8[14155776]{0:T(1024)(128)(4,1)} %bitcast.178), calls=%async_computation.13 | async-start | bytes 3145728
  1034.8 21.1 %slice-start.13 = ((s8[14155776]{0:T(1024)(128)(4,1)}), s8[4194304]{0:T(1024)(128)(4,1)S(1)}, s32[]{:S(2)}) async-start(s8[14155776]{0:T(1024)(128)(4,1)} %bitcast.178), calls=%async_computation.14 | async-start | bytes 8388608
  1034.8 21.1 %slice-start.14 = ((s8[14155776]{0:T(1024)(128)(4,1)}), s8[4194304]{0:T(1024)(128)(4,1)S(1)}, s32[]{:S(2)}) async-start(s8[14155776]{0:T(1024)(128)(4,1)} %bitcast.178), calls=%async_computation.15 | async-start | bytes 8388608
  1042.0 7.3 copy-start.1
  1048.0 7.9 slice-start.15
  1050.4 12.7 %slice-start.8 = ((s8[14155776]{0:T(1024)(128)(4,1)}), s8[1572864]{0:T(1024)(128)(4,1)S(1)}, s32[]{:S(2)}) async-start(s8[14155776]{0:T(1024)(128)(4,1)} %bitcast.175), calls=%async_computation.9 | async-start | bytes 3145728
  1050.5 12.7 %slice-start.9 = ((s8[14155776]{0:T(1024)(128)(4,1)}), s8[4194304]{0:T(1024)(128)(4,1)S(1)}, s32[]{:S(2)}) async-start(s8[14155776]{0:T(1024)(128)(4,1)} %bitcast.175), calls=%async_computation.10 | async-start | bytes 8388608
  1055.9 7.2 slice-start.10
  1055.9 8.6 slice-start.11
  1055.9 15.7 %slice-start.4 = ((s8[14155776]{0:T(1024)(128)(4,1)}), s8[4194304]{0:T(1024)(128)(4,1)S(1)}, s32[]{:S(2)}) async-start(s8[14155776]{0:T(1024)(128)(4,1)} %bitcast.172), calls=%async_computation.5 | async-start | bytes 8388608
  1056.0 15.7 %slice-start.5 = ((s8[14155776]{0:T(1024)(128)(4,1)}), s8[4194304]{0:T(1024)(128)(4,1)S(1)}, s32[]{:S(2)}) async-start(s8[14155776]{0:T(1024)(128)(4,1)} %bitcast.172), calls=%async_computation.6 | async-start | bytes 8388608
  1064.5 8.9 slice-start.6
  1064.5 9.3 slice-start.7
Sparse Core Ops, SparseCore 0:
  14.0 45.3 all-reduce.2

commit v2 on v1

--- a/solution.py
+++ b/solution.py
@@ -91,16 +91,103 @@
     pl.semaphore_wait(barrier, len(devs))
 
 
-def reduce_kernel(wq, wk, wv, wo, gate, up, down, gtail, g_out, n_out, land_x, land_y, land_p,
-                  raw_p, raw_q, raw_o, got, fwd, stage_p, stage, own_in, own_g, norm_send, norm_land,
-                  s_x, s_y, s_p, r_x, r_y, r_p, l_p, l_q, l_o, l_got, l_fwd, l_own, l_g, l_t, s_n, r_n):
+FRONT = ((2, 0, 6, 3), (4, 0, 24, 24), (4, SEG_TILES, 24, 24), (5, 0, 24, 24), (5, SEG_TILES, 24, 24), (6, 0, 9, 9), (6, SEG_TILES, 9, 9))
+WIN = 27600
+WIN_ROWS = LOCAL_ROWS - WIN
+
+
+def adam(g, p, m, v, lr, decay):
+    m = BETA_ONE * m + (1.0 - BETA_ONE) * g
+    v = BETA_TWO * v + (1.0 - BETA_TWO) * g * g
+    direction = (m * (1.0 / BIAS_ONE)) / (jnp.sqrt(v * (1.0 / BIAS_TWO)) + ADAM_EPS)
+    return p - lr * (decay * p + direction), m, v
+
+
+def step_kernel(wq, wk, wv, wo, gate, up, down, g_attn, g_mlp, g_final, p_in, m_in, v_in, rate,
+                p_out, m_out, v_out, o_wq, o_wk, o_wv, o_wo, o_gate, o_up, o_down, o_attn, o_mlp, o_final, o_norm,
+                g_flat, land_x, land_y, land_p, land,
+                raw_p, raw_q, raw_o, got, fwd, stage_p, stage, own_in, own_g, norm_send, norm_land, n_out,
+                front_raw, front, front_land, tail_g, window, halo, window_g, gains_send, gains_land, coef_ref,
+                gb, st, pb, stage_u, cin, cout,
+                s_x, s_y, s_p, r_x, r_y, r_p, l_p, l_q, l_o, l_got, l_fwd, l_own, l_g, s_n, r_n,
+                l_front, s_front, r_front, l_win, s_win, r_win, l_tail, l_six, s_gain, r_gain,
+                su_x, su_y, su_p, ru_x, ru_y, ru_o, r_px, r_py, f_x, f_y, d_x, d_y, l_in, l_out, l_c, l_so):
     refs = (wq, wk, wv, wo, gate, up, down)
+    outs7 = (o_wq, o_wk, o_wv, o_wo, o_gate, o_up, o_down)
     me = lax.axis_index("dp")
     flip, partner, xn, yn, diag = neighbours(me)
-    greet((partner, xn, yn))
-    tail_copy = pltpu.make_async_copy(gtail, g_out.at[pl.ds(SEG_ROWS, TAIL)], l_t)
-    tail_copy.start()
+    others = [lax.rem(me + o, 8) for o in range(1, 8)]
+    shift = 6 * me
+    lr = rate[0]
+    ins, outs = (p_in, m_in, v_in), (p_out, m_out, v_out)
     n_out[...] = jnp.zeros_like(n_out)
+    window[...] = jnp.zeros_like(window)
+    window_g[...] = jnp.zeros_like(window_g)
+    halo[:, pl.ds(56, 48), :] = jnp.zeros((3, 48, LANES), jnp.float32)
+    front[7] = jnp.zeros(front.shape[1:], jnp.float32)
+    greet(others)
+
+    def window_copies():
+        out = []
+        for a in range(3):
+            out.append(pltpu.make_async_copy(ins[a].at[pl.ds(WIN, 48)], window.at[a, pl.ds(0, 48)], l_win.at[a]))
+            out.append(pltpu.make_async_copy(ins[a].at[pl.ds(SEG_ROWS, 6)], window.at[a, pl.ds(48, 6)], l_win.at[3 + a]))
+        return out
+
+    def front_copies():
+        return [pltpu.make_async_copy(refs[k].at[pl.ds(off, cnt)], front_raw.at[d, pl.ds(0, cnt)], l_front.at[d])
+                for d, (k, off, cnt, width) in enumerate(FRONT)]
+
+    def front_sends():
+        return [remote(front.at[dev, pl.ds(0, TAIL)], front_land.at[o], s_front.at[o], r_front.at[o], dev) for o, dev in enumerate(others)]
+
+    def window_send():
+        return remote(window, halo.at[:, pl.ds(0, 56)], s_win, r_win, others[0])
+
+    def small_exchange():
+        for copy in window_copies() + front_copies():
+            copy.start()
+        rows = [(g_attn[0], 2), (g_mlp[0], 2), (g_final[...], 1)]
+        place = 0
+        for value, count in rows:
+            value = value.astype(jnp.float32)
+            for r in range(count):
+                for w in range(9):
+                    front[7, pl.ds(place, 1), :] = value[r:r + 1, w * LANES:(w + 1) * LANES]
+                    place += 1
+        for copy in window_copies() + front_copies():
+            copy.wait()
+        for d, (k, off, cnt, width) in enumerate(FRONT):
+            for t in range(cnt):
+                front[d, pl.ds(t // width * 8 * width + t % width, 8, stride=width), :] = front_raw[d, t].astype(jnp.float32)
+        window_send().start()
+        for copy in front_sends():
+            copy.start()
+
+    def small_finish():
+        total = front[me, pl.ds(0, TAIL), :]
+        for o, copy in enumerate(front_sends()):
+            copy.wait()
+            total = total + front_land[o]
+        window_send().wait()
+        total = total * 0.125
+        tail_g[...] = total
+
+        @pl.when(me == 7)
+        def _():
+            n_out[...] += jnp.sum((total * total).reshape(TAIL // 8, 8, LANES), axis=0)
+        copy = pltpu.make_async_copy(tail_g, g_flat.at[pl.ds(SEG_ROWS, TAIL)], l_tail)
+        copy.start()
+        copy.wait()
+
+    def state_loads(s):
+        row = pl.multiple_of(s * ROWS, 8)
+        for a in range(3):
+            pltpu.make_async_copy(ins[a].at[pl.ds(row, ROWS)], st.at[a], l_in.at[a]).start()
+
+    def gradient_load(s):
+        row = pl.multiple_of(s * ROWS, 8)
+        pltpu.make_async_copy(g_flat.at[pl.ds(row, ROWS + TAIL)], gb, l_in.at[3]).start()
 
     def job(s, link):
         j = lax.rem(s, HALF)
@@ -138,7 +225,6 @@
     def step(s, count):
         j = lax.rem(s, HALF)
         more = s < 23
-        own_give = (s >= 23) & (s < 31)
 
         @pl.when(more)
         def _():
@@ -182,6 +268,9 @@
                         stage[ring, a, d] = raw_q[a, d].astype(jnp.float32) + got[a, d] + fwd[a, d]
                     tiles_loop(add)
                 copies[a].start()
+
+        pl.when(s == 2)(small_exchange)
+        pl.when(s == 20)(small_finish)
 
         @pl.when((s >= 12) & (s < 20))
         def _():
@@ -230,7 +319,7 @@
             for a in range(3):
                 fetched(land_p.at[0], own_in.at[h, a], l_own.at[h, a])
             row = pl.multiple_of(tile * 8, 8)
-            out = pltpu.make_async_copy(own_g.at[h], g_out.at[pl.ds(row, ROWS)], l_g.at[h])
+            out = pltpu.make_async_copy(own_g.at[h], g_flat.at[pl.ds(row, ROWS)], l_g.at[h])
             pl.when(j >= 1)(out.wait)
 
             def relay(width, h=h):
@@ -247,33 +336,73 @@
 
     lax.fori_loop(0, 24 + LAG, step, 0)
 
+    state_loads(0)
+
     for r, dev in enumerate((partner, xn, yn)):
         norm_send[r] = n_out[...]
         copy = remote(norm_send.at[r], norm_land.at[r], s_n.at[r], r_n.at[r], dev)
         copy.start()
         copy.wait()
         n_out[...] += norm_land[r]
-    tail_copy.wait()
+    for h in (0, 1):
+        pltpu.make_async_copy(own_g.at[h], g_flat.at[pl.ds(0, ROWS)], l_g.at[h]).wait()
+    gradient_load(0)
+    norm = jnp.sqrt(jnp.sum(n_out[...], axis=(0, 1), keepdims=True))
+    o_norm[...] = jnp.broadcast_to(norm, (8, LANES))
+    coef_ref[...] = jnp.broadcast_to(jnp.minimum(1.0, MAX_NORM / (norm + CLIP_EPS)), (8, LANES))
+    copy = pltpu.make_async_copy(g_flat.at[pl.ds(WIN, 96)], window_g.at[pl.ds(0, 96)], l_tail)
+    copy.start()
+    copy.wait()
+    coef = coef_ref[pl.ds(0, 1), :]
+
+    def state_tail():
+        place = lax.broadcasted_iota(jnp.int32, (56, LANES), 0) + (me * LOCAL_ROWS + WIN)
+        decay = jnp.where(place < MATRIX_ROWS, WEIGHT_DECAY, 0.0)
+        new = adam(window_g[pl.ds(shift, 56), :] * coef, window[0], window[1], window[2], lr, decay)
+        for a in range(3):
+            window[a] = new[a]
+        gains_send[...] = new[0]
+        for a in range(3):
+            pltpu.make_async_copy(window.at[a, pl.ds(48, 6)], outs[a].at[pl.ds(SEG_ROWS, 6)], l_six.at[a]).start()
+
+        @pl.when(me == 7)
+        def _():
+            for o, dev in enumerate(others):
+                remote(gains_send, gains_land, s_gain.at[o], r_gain, dev).start()
+
+    def gains_finish():
+        def write(src):
+            t = src[...]
+
+            def row(first):
+                return jnp.concatenate([t[first + w:first + w + 1, :] for w in range(9)], axis=1)
+            o_attn[...] = jnp.concatenate([row(6), row(15)], axis=0).astype(jnp.bfloat16)
+            o_mlp[...] = jnp.concatenate([row(24), row(33)], axis=0).astype(jnp.bfloat16)
+            o_final[...] = row(42).astype(jnp.bfloat16)
+
+        @pl.when(me == 7)
+        def _():
+            for o, dev in enumerate(others):
+                remote(gains_send, gains_land, s_gain.at[o], r_gain, dev).wait_send()
+            write(gains_send)
+
+        @pl.when(me != 7)
+        def _():
+            remote(gains_send, gains_land, s_gain.at[0], r_gain, others[0]).wait_recv()
+            write(gains_land)
+        for a in range(3):
+            pltpu.make_async_copy(window.at[a, pl.ds(48, 6)], outs[a].at[pl.ds(SEG_ROWS, 6)], l_six.at[a]).wait()
+
+    def first_rows():
+        part = pl.ds(54 - shift, TAIL)
+        pb[pl.ds(0, TAIL), :] = adam(gb[pl.ds(0, TAIL), :] * coef, halo[0, part, :], halo[1, part, :], halo[2, part, :], lr, WEIGHT_DECAY)[0]
+
     for a in (0, 1):
         for par in range(3):
             remote(stage_p.at[par, a], land_p.at[0], s_p.at[par, a], r_p.at[0], partner).wait_send()
-        pltpu.make_async_copy(own_g.at[a], g_out.at[pl.ds(0, ROWS)], l_g.at[a]).wait()
     for ring in range(RING):
         remote(stage.at[ring, 0], land_x.at[0], s_x.at[ring], r_x.at[0], xn).wait_send()
         remote(stage.at[ring, 1], land_y.at[0], s_y.at[ring], r_y.at[0], yn).wait_send()
-
-
-def gather_kernel(g_in, p_in, m_in, v_in, head, scal, p_out, m_out, v_out, wq, wk, wv, wo, gate, up, down, land,
-                  gb, st, pb, stage, cin, cout, s_x, s_y, s_p, r_x, r_y, r_o, r_px, r_py, f_x, f_y, d_x, d_y,
-                  l_in, l_out, l_c, l_o):
-    refs = (wq, wk, wv, wo, gate, up, down)
-    me = lax.axis_index("dp")
-    flip, partner, xn, yn, diag = neighbours(me)
-    greet((partner, xn, yn))
-    coef, lr = scal[0], scal[1]
-    shift = 6 * me
-    pb[pl.ds(0, TAIL), :] = head[...]
-    ins, outs = (p_in, m_in, v_in), (p_out, m_out, v_out)
 
     def at(seg, c):
         return land.at[seg, pl.ds(pl.multiple_of(c * N, N), N)]
@@ -286,29 +415,26 @@
     def own(s):
         ring = lax.rem(s, RING)
         row = pl.multiple_of(s * ROWS, 8)
-        pltpu.make_async_copy(g_in.at[pl.ds(row, ROWS + TAIL)], gb, l_in.at[3]).start()
-        for a in range(3):
-            @pl.when(s >= 1)
-            def _(a=a):
+
+        @pl.when(s >= 1)
+        def _():
+            gradient_load(s)
+            for a in range(3):
                 pltpu.make_async_copy(st.at[a], outs[a].at[pl.ds(row, ROWS)], l_out.at[a]).wait()
-            pltpu.make_async_copy(ins[a].at[pl.ds(row, ROWS)], st.at[a], l_in.at[a]).start()
-        pltpu.make_async_copy(g_in.at[pl.ds(row, ROWS + TAIL)], gb, l_in.at[3]).wait()
+            state_loads(s)
+        pltpu.make_async_copy(g_flat.at[pl.ds(row, ROWS + TAIL)], gb, l_in.at[3]).wait()
         for a in range(3):
             pltpu.make_async_copy(ins[a].at[pl.ds(row, ROWS)], st.at[a], l_in.at[a]).wait()
+        pl.when(s == 0)(first_rows)
         slab = 48
         base = me * LOCAL_ROWS + s * ROWS
 
         def update(i, carry):
             d = pl.ds(pl.multiple_of(i * slab, 8), slab)
             e = pl.ds(i * slab + shift, slab)
-            g = gb[e, :] * coef
-            p = st[0, d, :]
-            m = BETA_ONE * st[1, d, :] + (1.0 - BETA_ONE) * g
-            v = BETA_TWO * st[2, d, :] + (1.0 - BETA_TWO) * g * g
-            direction = (m * (1.0 / BIAS_ONE)) / (jnp.sqrt(v * (1.0 / BIAS_TWO)) + ADAM_EPS)
             place = lax.broadcasted_iota(jnp.int32, (slab, LANES), 0) + (base + i * slab)
-            decay = jnp.where(place < MATRIX_ROWS, WEIGHT_DECAY * p, 0.0)
-            p = p - lr * (decay + direction)
+            decay = jnp.where(place < MATRIX_ROWS, WEIGHT_DECAY, 0.0)
+            p, m, v = adam(gb[e, :] * coef, st[0, d, :], st[1, d, :], st[2, d, :], lr, decay)
             st[0, d, :] = p
             st[1, d, :] = m
             st[2, d, :] = v
@@ -317,9 +443,9 @@
         lax.fori_loop(0, ROWS // slab, update, 0)
         for a in range(3):
             pltpu.make_async_copy(st.at[a], outs[a].at[pl.ds(row, ROWS)], l_out.at[a]).start()
-        copies = [remote(stage.at[ring], at(me, s), s_x.at[ring], r_x.at[s], xn),
-                  remote(stage.at[ring], at(me, s), s_y.at[ring], r_y.at[s], yn),
-                  remote(stage.at[ring], at(me, s), s_p.at[ring], r_o.at[s], partner)]
+        copies = [remote(stage_u.at[ring], at(me, s), su_x.at[ring], ru_x.at[s], xn),
+                  remote(stage_u.at[ring], at(me, s), su_y.at[ring], ru_y.at[s], yn),
+                  remote(stage_u.at[ring], at(me, s), su_p.at[ring], ru_o.at[s], partner)]
 
         @pl.when(s >= RING)
         def _():
@@ -330,7 +456,7 @@
             def body(r, carry):
                 for w in range(width):
                     t = r * width + w
-                    stage[ring, t] = pb[pl.ds(r * (8 * width) + w, 8, stride=width), :]
+                    stage_u[ring, t] = pb[pl.ds(r * (8 * width) + w, 8, stride=width), :]
                 return carry
             lax.fori_loop(0, N // width, body, 0)
         on_width(me, s * N, relay)
@@ -339,9 +465,9 @@
             copy.start()
 
         def conv(d):
-            cout[0, d] = stage[ring, d].astype(jnp.bfloat16)
+            cout[0, d] = stage_u[ring, d].astype(jnp.bfloat16)
         tiles_loop(conv)
-        store_piece(refs, me, s * N, cout.at[0], l_o.at[0])
+        store_piece(outs7, me, s * N, cout.at[0], l_so.at[0])
 
     def convert(slot, seg, chunk):
         pltpu.make_async_copy(at(0, 0), cin.at[slot - 1], l_c.at[slot - 1]).wait()
@@ -349,16 +475,17 @@
         def conv(d):
             cout[slot, d] = cin[slot - 1, d].astype(jnp.bfloat16)
         tiles_loop(conv)
-        store_piece(refs, seg, chunk * N, cout.at[slot], l_o.at[slot])
+        store_piece(outs7, seg, chunk * N, cout.at[slot], l_so.at[slot])
 
     def fetch(slot, seg, chunk):
         pltpu.make_async_copy(at(seg, chunk), cin.at[slot - 1], l_c.at[slot - 1]).start()
 
     def stored(slot):
-        pltpu.make_async_copy(cout.at[slot], wq.at[pl.ds(0, N)], l_o.at[slot]).wait()
-
-    def step(s, carry):
+        pltpu.make_async_copy(cout.at[slot], o_wq.at[pl.ds(0, N)], l_so.at[slot]).wait()
+
+    def gather_step(s, carry):
         j = s - 16
+        pl.when(s == 2)(state_tail)
         q = s - LAG
         q2 = s - LAG - 1
 
@@ -372,8 +499,8 @@
 
         @pl.when((s >= 16) & (s < 24))
         def _():
-            remote(at(xn, j), at(xn, j), f_y.at[j], r_y.at[s], yn).start()
-            remote(at(yn, 8 + j), at(yn, 8 + j), f_x.at[j], r_x.at[s], xn).start()
+            remote(at(xn, j), at(xn, j), f_y.at[j], ru_y.at[s], yn).start()
+            remote(at(yn, 8 + j), at(yn, 8 + j), f_x.at[j], ru_x.at[s], xn).start()
 
         @pl.when((q >= 1) & (q <= 24))
         def _():
@@ -395,12 +522,12 @@
 
         @pl.when((q >= 0) & (q < 24))
         def _():
-            remote(at(xseg, xc), at(xseg, xc), d_x.at[par], r_x.at[q], xn).wait_recv()
+            remote(at(xseg, xc), at(xseg, xc), d_x.at[par], ru_x.at[q], xn).wait_recv()
             copy = remote(at(xseg, xc), at(xseg, xc), d_x.at[par], r_px.at[q], partner)
             pl.when(q >= 2)(copy.wait_send)
             copy.start()
             fetch(1, xseg, xc)
-            remote(at(yseg, yc), at(yseg, yc), d_y.at[par], r_y.at[q], yn).wait_recv()
+            remote(at(yseg, yc), at(yseg, yc), d_y.at[par], ru_y.at[q], yn).wait_recv()
             copy = remote(at(yseg, yc), at(yseg, yc), d_y.at[par], r_py.at[q], partner)
             pl.when(q >= 2)(copy.wait_send)
             copy.start()
@@ -411,7 +538,7 @@
 
         @pl.when((q2 >= 0) & (q2 < 16))
         def _():
-            remote(at(partner, q2), at(partner, q2), s_p.at[0], r_o.at[q2], partner).wait_recv()
+            remote(at(partner, q2), at(partner, q2), su_p.at[0], ru_o.at[q2], partner).wait_recv()
             fetch(5, partner, q2)
 
         @pl.when((q2 >= 0) & (q2 < 24))
@@ -436,18 +563,19 @@
             convert(4, pyseg + flip, pyc)
         return carry
 
-    lax.fori_loop(0, 24 + LAG + 1, step, 0)
+    lax.fori_loop(0, 24 + LAG + 1, gather_step, 0)
+    gains_finish()
     stored(3)
     stored(4)
     for a in range(3):
         pltpu.make_async_copy(st.at[a], outs[a].at[pl.ds(0, ROWS)], l_out.at[a]).wait()
     for ring in range(RING):
-        remote(stage.at[ring], at(me, 0), s_x.at[ring], r_x.at[0], xn).wait_send()
-        remote(stage.at[ring], at(me, 0), s_y.at[ring], r_y.at[0], yn).wait_send()
-        remote(stage.at[ring], at(me, 0), s_p.at[ring], r_o.at[0], partner).wait_send()
+        remote(stage_u.at[ring], at(me, 0), su_x.at[ring], ru_x.at[0], xn).wait_send()
+        remote(stage_u.at[ring], at(me, 0), su_y.at[ring], ru_y.at[0], yn).wait_send()
+        remote(stage_u.at[ring], at(me, 0), su_p.at[ring], ru_o.at[0], partner).wait_send()
     for j in range(HALF):
-        remote(at(0, 0), at(0, 0), f_y.at[j], r_y.at[0], yn).wait_send()
-        remote(at(0, 0), at(0, 0), f_x.at[j], r_x.at[0], xn).wait_send()
+        remote(at(0, 0), at(0, 0), f_y.at[j], ru_y.at[0], yn).wait_send()
+        remote(at(0, 0), at(0, 0), f_x.at[j], ru_x.at[0], xn).wait_send()
     for par in (0, 1):
         remote(at(0, 0), at(0, 0), d_x.at[par], r_px.at[0], partner).wait_send()
         remote(at(0, 0), at(0, 0), d_y.at[par], r_py.at[0], partner).wait_send()
@@ -473,85 +601,41 @@
     return t.reshape(lead // 8, cols // LANES, 8, LANES).transpose(0, 2, 1, 3).reshape(shape)
 
 
-def reduce_call(tiles, gtail):
+def local_step(*arrays):
+    grads = arrays[:10]
+    states = [a.reshape(LOCAL_ROWS, LANES) for a in arrays[10:13]]
     dma = pltpu.SemaphoreType.DMA
     chunk = (N, 8, LANES)
-    return pl.pallas_call(
-        reduce_kernel,
-        out_shape=[jax.ShapeDtypeStruct((SEG_ROWS + TAIL, LANES), F32), jax.ShapeDtypeStruct((8, LANES), F32),
-                   jax.ShapeDtypeStruct((24,) + chunk, F32), jax.ShapeDtypeStruct((24,) + chunk, F32),
-                   jax.ShapeDtypeStruct((64,) + chunk, F32)],
-        in_specs=[ANY] * 7 + [VMEM],
-        out_specs=[ANY, VMEM, ANY, ANY, ANY],
-        scratch_shapes=[pltpu.VMEM((2,) + chunk, BF16), pltpu.VMEM((2,) + chunk, BF16), pltpu.VMEM((2,) + chunk, BF16),
-                        pltpu.VMEM((2,) + chunk, F32), pltpu.VMEM((2,) + chunk, F32), pltpu.VMEM((3, 2) + chunk, F32),
-                        pltpu.VMEM((RING, 2) + chunk, F32), pltpu.VMEM((2, 3) + chunk, F32), pltpu.VMEM((2, ROWS, LANES), F32),
-                        pltpu.VMEM((3, 8, LANES), F32), pltpu.VMEM((3, 8, LANES), F32),
+    shape = jax.ShapeDtypeStruct
+    flat = shape((LOCAL_ROWS, LANES), F32)
+    tile_counts = (2592, 864, 864, 2592, 6912, 6912, 6912)
+    vm = pltpu.VMEM
+    res = pl.pallas_call(
+        step_kernel,
+        out_shape=[flat] * 3 + [shape((c, 8, LANES), BF16) for c in tile_counts]
+        + [shape((2, 1152), BF16), shape((2, 1152), BF16), shape((1, 1152), BF16), shape((8, LANES), F32),
+           shape((SEG_ROWS + TAIL, LANES), F32), shape((24,) + chunk, F32), shape((24,) + chunk, F32),
+           shape((64,) + chunk, F32), shape((8, SEG_TILES, 8, LANES), F32)],
+        in_specs=[ANY] * 7 + [VMEM] * 3 + [ANY] * 3 + [SMEM],
+        out_specs=[ANY] * 10 + [VMEM] * 4 + [ANY] * 5,
+        scratch_shapes=[vm((2,) + chunk, BF16), vm((2,) + chunk, BF16), vm((2,) + chunk, BF16),
+                        vm((2,) + chunk, F32), vm((2,) + chunk, F32), vm((3, 2) + chunk, F32),
+                        vm((RING, 2) + chunk, F32), vm((2, 3) + chunk, F32), vm((2, ROWS, LANES), F32),
+                        vm((3, 8, LANES), F32), vm((3, 8, LANES), F32), vm((8, LANES), F32),
+                        vm((7, 24, 8, LANES), BF16), vm((8, 192, LANES), F32), vm((7, TAIL, LANES), F32), vm((TAIL, LANES), F32),
+                        vm((3, 56, LANES), F32), vm((3, 104, LANES), F32), vm((104, LANES), F32), vm((56, LANES), F32), vm((56, LANES), F32), vm((8, LANES), F32),
+                        vm((ROWS + TAIL, LANES), F32), vm((3, ROWS, LANES), F32), vm((ROWS + TAIL, LANES), F32),
+                        vm((RING,) + chunk, F32), vm((5,) + chunk, F32), vm((6,) + chunk, BF16),
                         dma((RING,)), dma((RING,)), dma((3, 2)), dma((24,)), dma((24,)), dma((64,)),
-                        dma((2,)), dma((2,)), dma((2,)), dma((2,)), dma((2,)), dma((2, 3)), dma((2,)), dma, dma((3,)), dma((3,))],
-        compiler_params=pltpu.CompilerParams(collective_id=0, has_side_effects=True, vmem_limit_bytes=LIMIT),
-        name="reduce_grads",
-    )(*tiles, gtail)
-
-
-def gather_call(g, p, m, v, head, scal):
-    dma = pltpu.SemaphoreType.DMA
-    chunk = (N, 8, LANES)
-    flat = jax.ShapeDtypeStruct((LOCAL_ROWS, LANES), F32)
-    tile_counts = (2592, 864, 864, 2592, 6912, 6912, 6912)
-    return pl.pallas_call(
-        gather_kernel,
-        out_shape=[flat] * 3 + [jax.ShapeDtypeStruct((c, 8, LANES), BF16) for c in tile_counts]
-        + [jax.ShapeDtypeStruct((8, SEG_TILES, 8, LANES), F32)],
-        in_specs=[ANY] * 4 + [VMEM, SMEM],
-        out_specs=[ANY] * 11,
-        scratch_shapes=[pltpu.VMEM((ROWS + TAIL, LANES), F32), pltpu.VMEM((3, ROWS, LANES), F32), pltpu.VMEM((ROWS + TAIL, LANES), F32),
-                        pltpu.VMEM((RING,) + chunk, F32), pltpu.VMEM((5,) + chunk, F32), pltpu.VMEM((6,) + chunk, BF16),
+                        dma((2,)), dma((2,)), dma((2,)), dma((2,)), dma((2,)), dma((2, 3)), dma((2,)), dma((3,)), dma((3,)),
+                        dma((7,)), dma((7,)), dma((7,)), dma((6,)), dma, dma, dma, dma((3,)), dma((7,)), dma,
                         dma((RING,)), dma((RING,)), dma((RING,)), dma((24,)), dma((24,)), dma((16,)), dma((24,)), dma((24,)),
                         dma((HALF,)), dma((HALF,)), dma((2,)), dma((2,)), dma((4,)), dma((3,)), dma((5,)), dma((6,))],
-        compiler_params=pltpu.CompilerParams(collective_id=1, has_side_effects=True, vmem_limit_bytes=LIMIT),
-        name="update_gather",
-    )(g, p, m, v, head, scal)
-
-
-def adam(g, p, m, v, lr, decay):
-    m = BETA_ONE * m + (1.0 - BETA_ONE) * g
-    v = BETA_TWO * v + (1.0 - BETA_TWO) * g * g
-    direction = (m / BIAS_ONE) / (jnp.sqrt(v / BIAS_TWO) + ADAM_EPS)
-    return p - lr * (decay * p + direction), m, v
-
-
-def local_step(*arrays):
-    grads = arrays[:10]
-    master, exp_avg, exp_avg_sq, lr = arrays[10:]
-    me = lax.axis_index("dp")
-    wq, wk, wv, wo, gate, up, down = grads[:7]
-    width = TAIL * LANES
-    gains = jnp.concatenate([g.reshape(-1) for g in grads[7:]] + [jnp.zeros((width - 5760,), BF16)])
-    firsts = [wv[0, 0, :16], gate[0, 0, :2], gate[0, 1, :2], up[0, 0, :2], up[0, 1, :2], down[0, 0, :6], down[0, 1, :6]]
-    heads = jnp.stack([f.reshape(-1)[:width] for f in firsts] + [gains]).astype(F32) * 0.125
-    gt = lax.psum(heads, "dp").reshape(8, TAIL, LANES)
-    window = jnp.stack([a[-width:] for a in (master, exp_avg, exp_avg_sq)])
-    window = jnp.pad(window, ((0, 0), (0, width)))
-    window = lax.dynamic_slice(window, (0, (42 - 6 * me) * LANES), (3, width))
-    tails = lax.all_gather(window, "dp").reshape(8, 3, TAIL, LANES)
-    gtail = lax.dynamic_index_in_dim(gt, me, 0, keepdims=False)
-
-    g, squares = reduce_call([to_tiles(x) for x in grads[:7]], gtail)[:2]
-    norm = jnp.sqrt(jnp.sum(squares) + jnp.sum(gt[7] * gt[7]))
-    coef = jnp.minimum(1.0, MAX_NORM / (norm + CLIP_EPS))
-    decay = jnp.where(lax.broadcasted_iota(jnp.int32, (8, TAIL, LANES), 0) < 7, WEIGHT_DECAY, 0.0)
-    new_tails = adam(coef * gt, tails[:, 0], tails[:, 1], tails[:, 2], lr, decay)
-    head = lax.dynamic_index_in_dim(new_tails[0], lax.rem(me + 7, 8), 0, keepdims=False)
-    res = gather_call(g, *[a.reshape(LOCAL_ROWS, LANES) for a in (master, exp_avg, exp_avg_sq)], head, jnp.stack([coef, lr]))
-    states = []
-    for full, tail in zip(res[:3], new_tails):
-        last = lax.dynamic_slice(tail, (me, 6 * me, 0), (1, 6, LANES))[0]
-        states.append(lax.dynamic_update_slice(full, last, (SEG_ROWS, 0)).reshape(-1))
+        compiler_params=pltpu.CompilerParams(collective_id=0, has_side_effects=True, vmem_limit_bytes=LIMIT),
+        name="adamw_step",
+    )(*[to_tiles(x) for x in grads[:7]], *grads[7:], *states, arrays[13].reshape(1))
     params = [from_tiles(t, x.shape[1:]) for t, x in zip(res[3:10], grads[:7])]
-    gains = new_tails[0][7].reshape(-1).astype(BF16)
-    params += [gains[:2304].reshape(2, 1152), gains[2304:4608].reshape(2, 1152), gains[4608:5760]]
-    return tuple(states + params + [norm])
+    return tuple([a.reshape(-1) for a in res[:3]] + params + [res[10], res[11], res[12].reshape(-1), res[13][0, 0]])
 
 
 def solution(mesh):

time: 1090 us -> 1020 us (0.936)
  waiting for transfers between devices: 25.7 us -> 0 us
  blocking collectives: 16.3 us -> 0 us
  between operations: 17.5 us -> 1.39 us
    psum x1 -> x0, waiting for transfers between devices: 25.7 us -> none  [local_step(): gt = lax.psum(heads, 'dp').reshape(8, TAIL, LANES)]
    all_gather x1 -> x0, blocking collectives: 16.3 us -> none  [local_step(): tails = lax.all_gather(window, 'dp').reshape(8, 3, TAIL, LANES)]
    pallas_call x2 -> x1, Pallas kernels: 943 us -> 946 us  [local_step(): pl.pallas_call(step_kernel, out_shape=[flat] * 3 + [shape((c, 8, LANES),...]
    unnamed x59 -> x54, local copies, waits for them, and re-layouts: 71.1 us -> 68.9 us
  transfers between devices with their start and end apart: 1 -> 0, of which waited for: 1 -> 0; matrix products, arithmetic and copies ran while one was open for 0% -> 0% of each run, Pallas kernels for 0% -> 0%
where the time goes in v2:
time: 1020 us
  Pallas kernels  946 us (93%)
  local copies, waits for them, and re-layouts  70.1 us (7%)
    pallas_call x1, Pallas kernels, local_step(): pl.pallas_call(step_kernel, out_shape=[flat] * 3 + [shape((c, 8, LANES),...  946 us
    unnamed x54, local copies, waits for them, and re-layouts  68.9 us

profile of v2, /device:TPU:0, one launch (start us, length us, event | category | flops | bytes accessed | tf_op | source)
XLA Modules:
  0.0 1019.0 jit_solution(5998457062846110983)
XLA Ops:
  1.3 946.2 %adamw_step.1 = (f32[27654,128]{1,0:T(8,128)}, f32[27654,128]{1,0:T(8,128)}, f32[27654,128]{1,0:T(8,128)}, bf16[2592,8,128]{2,1,0:T(8,128)(2,1)}, bf16[864,8,128...) custom-call(bf16[2592,8,128]{2,1,0:T(8,128)(2,1)} %bitcast.101, ...), custom_call_target="tpu_custom_call" | custom-call | tf_op jit(solution)/shard_map/adamw_step/pallas_call | solution.py:613
  947.5 1.2 slice.3
  948.7 1.3 reduce
  950.0 0.0 copy-start
  950.0 0.0 slice-start
  950.0 0.0 slice-start.1
  950.0 0.0 slice-start.2
  950.0 11.8 %copy.41 = f32[3539712]{0:T(1024)} copy(f32[3539712]{0:T(1024)} %bitcast.86) | data formatting | bytes 28317696
  961.8 2.5 copy-done
  964.2 0.0 slice-start.3
  964.2 7.2 copy.42
  971.4 0.0 slice-done
  971.4 0.0 slice-done.1
  971.4 1.3 slice-done.2
  972.7 0.7 slice-done.3
  973.4 0.0 copy-start.2
  973.4 0.0 slice-start.12
  973.4 0.0 slice-start.13
  973.4 7.2 copy.43
  980.6 6.1 copy.44
  986.8 0.0 copy-done.2
  986.8 1.2 copy.45
  988.0 0.0 copy-done.1
  988.0 1.2 copy.46
  989.2 5.4 copy.47
  994.6 0.0 slice-done.12
  994.6 0.0 slice-done.13
  994.6 0.0 slice-done.14
  994.6 0.0 slice-done.15
  994.7 0.0 slice-start.10
  994.7 0.0 slice-start.11
  994.7 0.0 slice-start.4
  994.7 0.0 slice-start.5
  994.7 7.2 copy.48
  1001.9 0.0 slice-done.8
  1001.9 0.0 slice-done.9
  1001.9 0.0 slice-done.10
  1001.9 1.4 slice-done.11
  1003.2 7.2 copy.49
  1010.4 0.0 slice-done.4
  1010.4 0.0 slice-done.5
  1010.4 1.7 slice-done.6
  1012.2 0.4 slice-done.7
  1012.6 5.3 copy.50
  1017.9 0.0 copy-done.4
  1017.9 0.6 copy.51
  1018.5 0.0 copy-done.3
  1018.5 0.6 copy.52
  (13 shorter events, 0.0 us)
Async XLA Ops:
  950.0 14.2 %copy-start = (f32[27654,128]{1,0:T(8,128)S(1)}, f32[27654,128]{1,0:T(8,128)}, u32[]{:S(2)}) copy-start(f32[27654,128]{1,0:T(8,128)} %get-tuple-element.29) | copy-start | bytes 42476548
  950.0 21.4 %slice-start = ((s8[14159872]{0:T(1024)(128)(4,1)}), s8[4194304]{0:T(1024)(128)(4,1)S(1)}, s32[]{:S(2)}) async-start(s8[14159872]{0:T(1024)(128)(4,1)} %bitcast.82), calls=%async_computation | async-start | bytes 8388608
  950.0 21.4 %slice-start.1 = ((s8[14159872]{0:T(1024)(128)(4,1)}), s8[4194304]{0:T(1024)(128)(4,1)S(1)}, s32[]{:S(2)}) async-start(s8[14159872]{0:T(1024)(128)(4,1)} %bitcast.82), calls=%async_computation.1 | async-start | bytes 8388608
  950.0 22.7 %slice-start.2 = ((s8[14159872]{0:T(1024)(128)(4,1)}), s8[4194304]{0:T(1024)(128)(4,1)S(1)}, s32[]{:S(2)}) async-start(s8[14159872]{0:T(1024)(128)(4,1)} %bitcast.82), calls=%async_computation.2 | async-start | bytes 8388608
  964.2 9.1 slice-start.3
  973.4 13.4 %copy-start.2 = (bf16[864,8,128]{2,1,0:T(8,128)(2,1)S(1)}, bf16[864,8,128]{2,1,0:T(8,128)(2,1)}, u32[]{:S(2)}) copy-start(bf16[864,8,128]{2,1,0:T(8,128)(2,1)} %get-tuple-element.32) | copy-start | bytes 5308420
  973.4 21.2 %slice-start.12 = ((s8[14155776]{0:T(1024)(128)(4,1)}), s8[4194304]{0:T(1024)(128)(4,1)S(1)}, s32[]{:S(2)}) async-start(s8[14155776]{0:T(1024)(128)(4,1)} %bitcast.96), calls=%async_computation.12 | async-start | bytes 8388608
  973.4 21.2 %slice-start.13 = ((s8[14155776]{0:T(1024)(128)(4,1)}), s8[4194304]{0:T(1024)(128)(4,1)S(1)}, s32[]{:S(2)}) async-start(s8[14155776]{0:T(1024)(128)(4,1)} %bitcast.96), calls=%async_computation.13 | async-start | bytes 8388608
  973.4 21.2 %slice-start.14 = ((s8[14155776]{0:T(1024)(128)(4,1)}), s8[4194304]{0:T(1024)(128)(4,1)S(1)}, s32[]{:S(2)}) async-start(s8[14155776]{0:T(1024)(128)(4,1)} %bitcast.96), calls=%async_computation.14 | async-start | bytes 8388608
  980.6 7.4 copy-start.1
  986.8 7.9 slice-start.15
  989.2 12.7 %slice-start.8 = ((s8[14155776]{0:T(1024)(128)(4,1)}), s8[1572864]{0:T(1024)(128)(4,1)S(1)}, s32[]{:S(2)}) async-start(s8[14155776]{0:T(1024)(128)(4,1)} %bitcast.93), calls=%async_computation.8 | async-start | bytes 3145728
  989.2 12.7 %slice-start.9 = ((s8[14155776]{0:T(1024)(128)(4,1)}), s8[4194304]{0:T(1024)(128)(4,1)S(1)}, s32[]{:S(2)}) async-start(s8[14155776]{0:T(1024)(128)(4,1)} %bitcast.93), calls=%async_computation.9 | async-start | bytes 8388608
  994.7 7.2 slice-start.10
  994.7 8.6 slice-start.11
  994.7 15.7 %slice-start.4 = ((s8[14155776]{0:T(1024)(128)(4,1)}), s8[4194304]{0:T(1024)(128)(4,1)S(1)}, s32[]{:S(2)}) async-start(s8[14155776]{0:T(1024)(128)(4,1)} %bitcast.90), calls=%async_computation.4 | async-start | bytes 8388608
  994.7 15.7 %slice-start.5 = ((s8[14155776]{0:T(1024)(128)(4,1)}), s8[4194304]{0:T(1024)(128)(4,1)S(1)}, s32[]{:S(2)}) async-start(s8[14155776]{0:T(1024)(128)(4,1)} %bitcast.90), calls=%async_computation.5 | async-start | bytes 8388608
  1003.2 8.9 slice-start.6
  1003.2 9.3 slice-start.7
  1012.6 5.3 copy-start.4
  1012.6 5.9 copy-start.3

commit v3 on v0

v3 whole, which is shorter than its diff:
```python
import functools
import jax
import jax.numpy as jnp
from jax import lax
from jax.experimental import pallas as pl
from jax.experimental.pallas import tpu as pltpu
from jax.sharding import PartitionSpec as P

BETA_ONE = 0.9
BETA_TWO = 0.95
ADAM_EPS = 1e-8
WEIGHT_DECAY = 0.1
MAX_NORM = 1.0
CLIP_EPS = 1e-6
STEP = 4
BIAS_ONE = 1.0 - BETA_ONE ** STEP
BIAS_TWO = 1.0 - BETA_TWO ** STEP

MESH = pl.DeviceIdType.MESH
F32 = jnp.float32
BF16 = jnp.bfloat16
LANES = 128
SEG_TILES = 3456
SEG_ROWS = SEG_TILES * 8
LOCAL_ROWS = SEG_ROWS + 6
MATRIX_ROWS = 8 * SEG_ROWS
TAIL = 48
WIN = 27600
N = 216
ROWS = N * 8
HALF = SEG_TILES // 2 // N
BOTH = 2 * HALF
SLOTS = 3 * HALF
LATE = 3
RING = 4
LAG = 5
COUNTS = (2592, 864, 864, 2592, 6912, 6912, 6912)
FRONT = ((2, 0, 6, 3),) + tuple((k, t, 24, 24) for k in (4, 5) for t in (0, SEG_TILES)) + tuple((6, t, 9, 9) for t in (0, SEG_TILES))
LIMIT = 62 * 1024 * 1024


def neighbours(me):
    core = lax.rem(me, 2)
    x = lax.rem(lax.div(me, 2), 2)
    y = lax.div(me, 4)
    flip = 1 - 2 * core
    xn = me + 2 - 4 * x
    yn = me + 4 - 8 * y
    diag = xn + 4 - 8 * y
    return flip, me + flip, xn, yn, diag


def on_piece(refs, seg, tile, act):
    wq, wk, wv, wo, gate, up, down = refs
    pl.when((seg == 0) & (tile < 2592))(lambda: act(wq, tile))
    pl.when((seg == 0) & (tile >= 2592))(lambda: act(wk, tile - 2592))
    pl.when((seg == 1) & (tile < 864))(lambda: act(wv, tile))
    pl.when((seg == 1) & (tile >= 864))(lambda: act(wo, tile - 864))
    pl.when((seg == 2) | (seg == 3))(lambda: act(gate, (seg - 2) * SEG_TILES + tile))
    pl.when((seg == 4) | (seg == 5))(lambda: act(up, (seg - 4) * SEG_TILES + tile))
    pl.when((seg == 6) | (seg == 7))(lambda: act(down, (seg - 6) * SEG_TILES + tile))


def on_width(seg, tile, act):
    narrow = ((seg == 0) & (tile >= 2592)) | ((seg == 1) & (tile < 864))
    wide = (seg >= 2) & (seg < 6)
    pl.when(wide)(lambda: act(24))
    pl.when(narrow)(lambda: act(3))
    pl.when(jnp.logical_not(wide | narrow))(lambda: act(9))


def load_piece(refs, seg, tile, buf, sem):
    def act(ref, off):
        pltpu.make_async_copy(ref.at[pl.ds(off, N)], buf, sem).start()
    on_piece(refs, seg, tile, act)


def store_piece(refs, seg, tile, buf, sem):
    def act(ref, off):
        pltpu.make_async_copy(buf, ref.at[pl.ds(off, N)], sem).start()
    on_piece(refs, seg, tile, act)


def tiles_loop(body, group=12):
    def step(i, carry):
        body(pl.ds(pl.multiple_of(i * group, group), group))
        return carry
    lax.fori_loop(0, N // group, step, 0)


def remote(src, dst, send, recv, dev):
    return pltpu.make_async_remote_copy(src_ref=src, dst_ref=dst, send_sem=send, recv_sem=recv, device_id=(dev,), device_id_type=MESH)


def greet(devs):
    barrier = pltpu.get_barrier_semaphore()
    for dev in devs:
        pl.semaphore_signal(barrier, inc=1, device_id=(dev,), device_id_type=MESH)
    pl.semaphore_wait(barrier, len(devs))


def adam(g, p, m, v, lr, decay):
    m = BETA_ONE * m + (1.0 - BETA_ONE) * g
    v = BETA_TWO * v + (1.0 - BETA_TWO) * g * g
    direction = (m * (1.0 / BIAS_ONE)) / (jnp.sqrt(v * (1.0 / BIAS_TWO)) + ADAM_EPS)
    return p - lr * (decay * p + direction), m, v


def local(src, dst, sem):
    return pltpu.make_async_copy(src, dst, sem)


def step_kernel(*args):
    refs, small, ins, rate = args[:7], args[7:10], args[10:13], args[13]
    outs, outs7, gains_out, o_norm = args[14:17], args[17:24], args[24:27], args[27]
    g_flat, land_l, land_p, land, spare_x, spare_y = args[28:34]
    (raw, stage_p, stage_u, aux, stage, own_in, own_g, norm_send, norm_land, n_out, front_raw, front, front_land, tail_g,
     window, halo, window_g, gains_send, gains_land, gb, st, pb, cin, cout) = args[34:58]
    (s_l, s_p, r_l, r_p, l_raw, l_aux, l_own, l_g, s_n, r_n, l_front, s_front, r_front, l_win, s_win, r_win, l_tail, l_six, s_gain, r_gain,
     su, ru, ru_o, r_d, s_f, s_d, l_in, l_out, l_c, l_so) = args[58:]
    spare = (spare_x, spare_y)
    me = lax.axis_index("dp")
    flip, partner, xn, yn, diag = neighbours(me)
    links = (xn, yn)
    pair = range(len(links))
    trio = range(len(ins))
    others = [lax.rem(me + o, 8) for o in range(1, 8)]
    shift = 6 * me
    lr = rate[0]
    n_out[...] = jnp.zeros_like(n_out)
    window[...] = jnp.zeros_like(window)
    window_g[...] = jnp.zeros_like(window_g)
    halo[:, pl.ds(56, TAIL), :] = jnp.zeros((3, TAIL, LANES), F32)
    front[7] = jnp.zeros(front.shape[1:], F32)
    greet(others)

    def raw_wait(kind, a):
        local(refs[0].at[pl.ds(0, N)], raw.at[kind, a], l_raw.at[kind, a]).wait()

    def to_partner(par, a, slot):
        return remote(stage_p.at[par, a], land_p.at[slot], s_p.at[par, a], r_p.at[slot], partner)

    def to_link(ring, a, slot):
        return remote(stage.at[ring, a], land_l.at[a, slot], s_l.at[ring, a], r_l.at[a, slot], links[a])

    def window_copies():
        out = []
        for a in trio:
            for row, place, rows in ((WIN, 0, TAIL), (SEG_ROWS, TAIL, 6)):
                out.append(local(ins[a].at[pl.ds(row, rows)], window.at[a, pl.ds(place, rows)], l_win.at[len(out)]))
        return out

    def front_copies():
        return [local(refs[k].at[pl.ds(off, cnt)], front_raw.at[d, pl.ds(0, cnt)], l_front.at[d]) for d, (k, off, cnt, width) in enumerate(FRONT)]

    def front_sends():
        return [remote(front.at[dev, pl.ds(0, TAIL)], front_land.at[o], s_front.at[o], r_front.at[o], dev) for o, dev in enumerate(others)]

    def window_send():
        return remote(window, halo.at[:, pl.ds(0, 56)], s_win, r_win, others[0])

    def small_exchange():
        for copy in window_copies() + front_copies():
            copy.start()
        place = 0
        for ref, count in zip(small, (2, 2, 1)):
            value = ref[...].reshape(count, 9 * LANES).astype(F32)
            for r in range(count):
                for w in range(9):
                    front[7, pl.ds(place, 1), :] = value[r:r + 1, w * LANES:(w + 1) * LANES]
                    place += 1
        for copy in window_copies() + front_copies():
            copy.wait()
        for d, (k, off, cnt, width) in enumerate(FRONT):
            for t in range(cnt):
                front[d, pl.ds(t // width * 8 * width + t % width, 8, stride=width), :] = front_raw[d, t].astype(F32)
        window_send().start()
        for copy in front_sends():
            copy.start()

    def small_finish():
        total = front[me, pl.ds(0, TAIL), :]
        for o, copy in enumerate(front_sends()):
            copy.wait()
            total = total + front_land[o]
        window_send().wait()
        total = total * 0.125
        tail_g[...] = total

        @pl.when(me == 7)
        def _():
            n_out[...] += jnp.sum((total * total).reshape(TAIL // 8, 8, LANES), axis=0)
        copy = local(tail_g, g_flat.at[pl.ds(SEG_ROWS, TAIL)], l_tail)
        copy.start()
        copy.wait()

    def link_jobs(s):
        jobs = []
        for a in pair:
            half = jnp.where(s < BOTH, a, 1 - a)
            seg = jnp.where(s < HALF, diag, links[a])
            jobs.append((seg, (half * HALF + lax.rem(s, HALF)) * N, a * SLOTS + s))
        return jobs

    def own_jobs(j):
        return [(me, (h * HALF + j) * N, 2 * SLOTS + h * HALF + j) for h in pair]

    def give(jobs, kind, par, wait_old):
        for a, (seg, tile, slot) in enumerate(jobs):
            load_piece(refs, seg + flip, tile, raw.at[kind, a], l_raw.at[kind, a])
        for a, (seg, tile, slot) in enumerate(jobs):
            raw_wait(kind, a)
            copy = to_partner(par, a, slot)
            pl.when(wait_old)(copy.wait_send)

            def conv(d, a=a):
                stage_p[par, a, d] = raw[kind, a, d].astype(F32)
            tiles_loop(conv)
            copy.start()

    def step(s, count):
        j = lax.rem(s, HALF)
        ring = lax.rem(s, RING)

        @pl.when(s < SLOTS - 1)
        def _():
            give(link_jobs(s + 1), 0, lax.rem(s + 1, 2), s >= 1)

        @pl.when(s < SLOTS)
        def _():
            jobs = link_jobs(s)
            for a, (seg, tile, slot) in enumerate(jobs):
                load_piece(refs, seg, tile, raw.at[1, a], l_raw.at[1, a])
            for a, (seg, tile, slot) in enumerate(jobs):
                to_partner(0, a, slot).wait_recv()
                local(land_p.at[slot], aux.at[0, a], l_aux.at[0, a]).start()

            @pl.when(s >= BOTH)
            def _():
                for a in pair:
                    to_link(0, a, j).wait_recv()
                for a in pair:
                    local(land_l.at[1 - a, j], aux.at[1, a], l_aux.at[1, a]).start()
            for a in pair:
                raw_wait(1, a)
                local(land_p.at[0], aux.at[0, a], l_aux.at[0, a]).wait()
                copy = to_link(ring, a, s)
                pl.when(s >= RING)(copy.wait_send)

                @pl.when(s < BOTH)
                def _(a=a):
                    def add(d):
                        stage[ring, a, d] = raw[1, a, d].astype(F32) + aux[0, a, d]
                    tiles_loop(add)

                @pl.when(s >= BOTH)
                def _(a=a):
                    local(land_p.at[0], aux.at[1, a], l_aux.at[1, a]).wait()

                    def add(d):
                        stage[ring, a, d] = raw[1, a, d].astype(F32) + aux[0, a, d] + aux[1, a, d]
                    tiles_loop(add)
                copy.start()

        pl.when(s == 2)(small_exchange)
        pl.when(s == BOTH + 4)(small_finish)

        @pl.when((s >= HALF + 4) & (s < BOTH + 4))
        def _():
            give(own_jobs(s - HALF - 4), 2, 2, s > HALF + 4)

        @pl.when(s >= BOTH + LAG)
        def _():
            take_own(s - BOTH - LAG)
        return count

    def take_own(j):
        for h, (seg, tile, slot) in enumerate(own_jobs(j)):
            load_piece(refs, seg, tile, raw.at[2, h], l_raw.at[2, h])
            to_partner(2, h, slot).wait_recv()
            local(land_p.at[slot], own_in.at[h, 0], l_own.at[h, 0]).start()
        for k in (1, 2):
            for h in pair:
                a = h if k == 1 else 1 - h
                slot = k * HALF + j
                to_link(0, a, slot).wait_recv()
                local(land_l.at[a, slot], own_in.at[h, k], l_own.at[h, k]).start()
        for h, (seg, tile, slot) in enumerate(own_jobs(j)):
            raw_wait(2, h)
            for a in trio:
                local(land_p.at[0], own_in.at[h, a], l_own.at[h, a]).wait()
            row = pl.multiple_of(tile * 8, 8)
            out = local(own_g.at[h], g_flat.at[pl.ds(row, ROWS)], l_g.at[h])
            pl.when(j >= 1)(out.wait)

            def relay(width, h=h):
                def body(r, acc):
                    for w in range(width):
                        t = r * width + w
                        g = (raw[2, h, t].astype(F32) + own_in[h, 0, t] + own_in[h, 1, t] + own_in[h, 2, t]) * 0.125
                        own_g[h, pl.ds(r * (8 * width) + w, 8, stride=width), :] = g
                        acc = acc + g * g
                    return acc
                n_out[...] += lax.fori_loop(0, N // width, body, jnp.zeros((8, LANES), F32))
            on_width(me, tile, relay)
            out.start()

    def state_loads(s):
        row = pl.multiple_of(s * ROWS, 8)
        for a in trio:
            local(ins[a].at[pl.ds(row, ROWS)], st.at[a], l_in.at[a]).start()

    def gradient_load(s):
        row = pl.multiple_of(s * ROWS, 8)
        return local(g_flat.at[pl.ds(row, ROWS + TAIL)], gb, l_in.at[3])

    give(link_jobs(0), 0, 0, False)
    lax.fori_loop(0, SLOTS + LAG, step, 0)
    state_loads(0)

    for r, dev in enumerate((partner, xn, yn)):
        norm_send[r] = n_out[...]
        copy = remote(norm_send.at[r], norm_land.at[r], s_n.at[r], r_n.at[r], dev)
        copy.start()
        copy.wait()
        n_out[...] += norm_land[r]
    for h in pair:
        local(own_g.at[h], g_flat.at[pl.ds(0, ROWS)], l_g.at[h]).wait()
    gradient_load(0).start()
    norm = jnp.sqrt(jnp.sum(n_out[...], axis=(0, 1), keepdims=True))
    o_norm[...] = jnp.broadcast_to(norm, (8, LANES))
    n_out[...] = jnp.broadcast_to(jnp.minimum(1.0, MAX_NORM / (norm + CLIP_EPS)), (8, LANES))
    coef = n_out[pl.ds(0, 1), :]
    for a in pair:
        for par in trio:
            to_partner(par, a, 0).wait_send()
        for ring in range(RING):
            to_link(ring, a, 0).wait_send()

    def state_tail():
        copy = local(g_flat.at[pl.ds(WIN, 2 * TAIL)], window_g.at[pl.ds(0, 2 * TAIL)], l_tail)
        copy.start()
        copy.wait()
        place = lax.broadcasted_iota(jnp.int32, (56, LANES), 0) + (me * LOCAL_ROWS + WIN)
        decay = jnp.where(place < MATRIX_ROWS, WEIGHT_DECAY, 0.0)
        new = adam(window_g[pl.ds(shift, 56), :] * coef, window[0], window[1], window[2], lr, decay)
        gains_send[...] = new[0]
        for a in trio:
            window[a] = new[a]
            six_store(a).start()

        @pl.when(me == 7)
        def _():
            for o, dev in enumerate(others):
                gains_copy(o, dev).start()

    def six_store(a):
        return local(window.at[a, pl.ds(TAIL, 6)], outs[a].at[pl.ds(SEG_ROWS, 6)], l_six.at[a])

    def gains_copy(o, dev):
        return remote(gains_send, gains_land, s_gain.at[o], r_gain, dev)

    def gains_finish():
        def write(src):
            t = src[...]

            def row(r):
                return jnp.concatenate([t[6 + 9 * r + w:7 + 9 * r + w, :] for w in range(9)], axis=1)
            for out, rows in zip(gains_out, ((0, 1), (2, 3), (4,))):
                out[...] = jnp.concatenate([row(r) for r in rows], axis=0).astype(BF16)

        @pl.when(me == 7)
        def _():
            for o, dev in enumerate(others):
                gains_copy(o, dev).wait_send()
            write(gains_send)

        @pl.when(me != 7)
        def _():
            gains_copy(0, others[0]).wait_recv()
            write(gains_land)
        for a in trio:
            six_store(a).wait()

    def first_rows():
        part = pl.ds(54 - shift, TAIL)
        pb[pl.ds(0, TAIL), :] = adam(gb[pl.ds(0, TAIL), :] * coef, halo[0, part, :], halo[1, part, :], halo[2, part, :], lr, WEIGHT_DECAY)[0]

    def at(seg, c):
        return land.at[seg, pl.ds(pl.multiple_of(c * N, N), N)]

    def place(a, seg, chunk, q, act):
        low = (1 + a) * HALF - LATE
        late = (q >= low) & (q < low + LATE)
        pl.when(late)(lambda: act(spare[a].at[pl.ds((q - low) * N, N)]))
        pl.when(jnp.logical_not(late))(lambda: act(at(seg, chunk)))

    def link_piece(q, a):
        direct = q < BOTH
        return jnp.where(direct, links[a], diag), jnp.where(direct, q, q - (1 + a) * HALF)

    def own(s):
        ring = lax.rem(s, RING)
        row = pl.multiple_of(s * ROWS, 8)

        def state_store(a):
            return local(st.at[a], outs[a].at[pl.ds(row, ROWS)], l_out.at[a])

        @pl.when(s >= 1)
        def _():
            gradient_load(s).start()
            for a in trio:
                state_store(a).wait()
            state_loads(s)
        gradient_load(s).wait()
        for a in trio:
            local(ins[a].at[pl.ds(row, ROWS)], st.at[a], l_in.at[a]).wait()
        pl.when(s == 0)(first_rows)
        slab = 48
        base = me * LOCAL_ROWS + s * ROWS

        def update(i, carry):
            d = pl.ds(pl.multiple_of(i * slab, 8), slab)
            e = pl.ds(i * slab + shift, slab)
            rows = lax.broadcasted_iota(jnp.int32, (slab, LANES), 0) + (base + i * slab)
            decay = jnp.where(rows < MATRIX_ROWS, WEIGHT_DECAY, 0.0)
            new = adam(gb[e, :] * coef, st[0, d, :], st[1, d, :], st[2, d, :], lr, decay)
            for a in trio:
                st[a, d, :] = new[a]
            pb[e, :] = new[0]
            return carry
        lax.fori_loop(0, ROWS // slab, update, 0)
        for a in trio:
            state_store(a).start()
        devs = links + (partner,)

        @pl.when(s >= RING)
        def _():
            for a in trio:
                remote(stage_u.at[ring], at(me, s), su.at[a, ring], ru_o.at[s], devs[a]).wait_send()

        def relay(width):
            def body(r, carry):
                for w in range(width):
                    stage_u[ring, r * width + w] = pb[pl.ds(r * (8 * width) + w, 8, stride=width), :]
                return carry
            lax.fori_loop(0, N // width, body, 0)
        on_width(me, s * N, relay)
        pb[pl.ds(0, TAIL), :] = pb[pl.ds(ROWS, TAIL), :]
        for a in pair:
            place(a, me, s, s, lambda ref, a=a: remote(stage_u.at[ring], ref, su.at[a, ring], ru.at[a, s], devs[a]).start())
        remote(stage_u.at[ring], at(me, s), su.at[2, ring], ru_o.at[s], partner).start()

        def conv(d):
            cout[5, d] = stage_u[ring, d].astype(BF16)
        tiles_loop(conv)
        store_piece(outs7, me, s * N, cout.at[5], l_so.at[5])

    def convert(k, seg, chunk):
        local(at(0, 0), cin.at[k], l_c.at[k]).wait()

        def conv(d):
            cout[k, d] = cin[k, d].astype(BF16)
        tiles_loop(conv)
        store_piece(outs7, seg, chunk * N, cout.at[k], l_so.at[k])

    def fetch(k, ref):
        local(ref, cin.at[k], l_c.at[k]).start()

    def stored(k):
        local(cout.at[k], outs7[0].at[pl.ds(0, N)], l_so.at[k]).wait()

    last = SLOTS - LATE

    def link_wait(a, q):
        return remote(at(0, 0), at(0, 0), s_d.at[a, 0], ru.at[a, q], links[a])

    def hand(a, par, q, src, dst):
        return remote(src, dst, s_d.at[a, par], r_d.at[a, q], partner)

    def forward(a, seg, chunk, j):
        return remote(at(seg, chunk), at(seg, chunk), s_f.at[a, j], ru.at[a, BOTH + j], links[a])

    def gather_step(s, carry):
        j = s - BOTH
        q = s - LAG
        z = q - 1
        par = lax.rem(s, 2)
        arrives = (q >= 0) & (q < last)
        from_partner = (z >= 0) & (z < last)
        own_partner = (z >= 0) & (z < BOTH)
        pl.when(s == 2)(state_tail)
        pl.when((s >= 1) & (s <= BOTH))(lambda: stored(5))
        pl.when(s < BOTH)(lambda: own(s))

        @pl.when((j >= 0) & (j < HALF - LATE))
        def _():
            forward(1, xn, j, j).start()
            forward(0, yn, HALF + j, j).start()

        @pl.when((q >= 1) & (q <= last))
        def _():
            for a in pair:
                stored(a)

        @pl.when((z >= 1) & (z <= last))
        def _():
            for a in pair:
                stored(2 + a)

        pl.when((z >= 1) & (z <= BOTH))(lambda: stored(4))

        @pl.when(arrives)
        def _():
            for a in pair:
                seg, chunk = link_piece(q, a)
                link_wait(a, q).wait_recv()
                pl.when(q >= 2)(hand(a, par, q, at(0, 0), at(0, 0)).wait_send)

                def act(ref, a=a, seg=seg, chunk=chunk):
                    hand(a, par, q, ref, at(seg, chunk)).start()
                    fetch(a, ref)
                place(a, seg, chunk, q, act)

        @pl.when(own_partner)
        def _():
            remote(at(0, 0), at(0, 0), su.at[2, 0], ru_o.at[z], partner).wait_recv()
            fetch(4, at(partner, z))

        @pl.when(from_partner)
        def _():
            for a in pair:
                seg, chunk = link_piece(z, a)
                hand(a, 0, z, at(0, 0), at(0, 0)).wait_recv()
                fetch(2 + a, at(seg + flip, chunk))

        @pl.when(arrives)
        def _():
            for a in pair:
                convert(a, *link_piece(q, a))

        pl.when(own_partner)(lambda: convert(4, partner, z))

        @pl.when(from_partner)
        def _():
            for a in pair:
                seg, chunk = link_piece(z, a)
                convert(2 + a, seg + flip, chunk)
        return carry

    lax.fori_loop(0, last + LAG + 1, gather_step, 0)
    gains_finish()
    for a in pair:
        stored(2 + a)
        for par in pair:
            hand(a, par, 0, at(0, 0), at(0, 0)).wait_send()
        for j in range(HALF - LATE):
            forward(a, 0, 0, j).wait_send()
    for a in trio:
        local(st.at[a], outs[a].at[pl.ds(0, ROWS)], l_out.at[a]).wait()
        for ring in range(RING):
            remote(stage_u.at[ring], at(me, 0), su.at[a, ring], ru_o.at[0], partner).wait_send()


def copy_kernel(*args):
    ins, outs, (wide, thin, l_in, l_out) = args[:10], args[10:20], args[20:]
    depth = wide.shape[0]
    jobs = []
    for src, dst in zip(ins, outs):
        size, kind = src.shape[0], len(src.shape) - 2
        piece = (SEG_ROWS // 8, COUNTS[1])[kind]
        for off in range(0, size, piece):
            rows = pl.ds(off, min(piece, size - off))
            n = len(jobs)
            buf = (wide, thin)[kind].at[n % depth, pl.ds(0, rows.size)]
            jobs.append((local(src.at[rows], buf, l_in.at[n % depth]), local(buf, dst.at[rows], l_out.at[n % depth])))
    ahead = depth // 2
    for n in range(len(jobs) + ahead):
        if n < len(jobs):
            if n >= depth:
                jobs[n - depth][1].wait()
            jobs[n][0].start()
        if n >= ahead:
            jobs[n - ahead][0].wait()
            jobs[n - ahead][1].start()
    for job in jobs[-depth:]:
        job[1].wait()


def late_kernel(mine, *args):
    came, outs7 = args[:2], args[9:16]
    cin, cout, l_in, l_out = args[16:]
    flip, partner, xn, yn, diag = neighbours(lax.axis_index("dp"))
    seg = diag if mine else diag + flip
    jobs = [(a, i, a * LATE + i) for a in range(2) for i in range(LATE)]
    loads = [local(came[a].at[pl.ds(i * N, N)], cin.at[k], l_in.at[k]) for a, i, k in jobs]
    for load in loads:
        load.start()
    for a, i, k in jobs:
        loads[k].wait()

        def conv(d, k=k):
            cout[k, d] = cin[k, d].astype(BF16)
        tiles_loop(conv)
        store_piece(outs7, seg, ((1 + a) * HALF - LATE + i) * N + 0 * seg, cout.at[k], l_out.at[k])
    for k in range(2 * LATE):
        local(cout.at[k], outs7[0].at[pl.ds(0, N)], l_out.at[k]).wait()


ANY = pl.BlockSpec(memory_space=pl.ANY)
VMEM = pl.BlockSpec(memory_space=pltpu.VMEM)
SMEM = pl.BlockSpec(memory_space=pltpu.SMEM)


def to_tiles(x):
    cols = x.shape[-1]
    lead = x.size // cols
    return x.reshape(lead // 8, 8, cols // LANES, LANES).transpose(0, 2, 1, 3).reshape(-1, 8, LANES)


def from_tiles(t, shape):
    cols = shape[-1]
    lead = t.size // cols
    return t.reshape(lead // 8, cols // LANES, 8, LANES).transpose(0, 2, 1, 3).reshape(shape)


def shapes(kind, dtype, *dims):
    return [kind(d, dtype) for d in dims]


def dmas(*dims):
    return [pltpu.SemaphoreType.DMA(d) if d else pltpu.SemaphoreType.DMA for d in dims]


def params_of(**kw):
    return pltpu.CompilerParams(vmem_limit_bytes=LIMIT, has_side_effects=True, **kw)


def copy_call(arrays):
    depth = 12
    moved = 2 * sum(a.size * a.dtype.itemsize for a in arrays)
    return pl.pallas_call(
        copy_kernel,
        out_shape=[jax.ShapeDtypeStruct(a.shape, a.dtype) for a in arrays],
        in_specs=[ANY] * 10,
        out_specs=[ANY] * 10,
        scratch_shapes=[pltpu.VMEM((depth, SEG_ROWS // 8, LANES), F32), pltpu.VMEM((depth, COUNTS[1], 8, LANES), BF16)] + dmas((depth,), (depth,)),
        compiler_params=params_of(),
        cost_estimate=pl.CostEstimate(flops=100 * moved, bytes_accessed=moved, transcendentals=0),
        name="copy_results",
    )(*arrays)


def late_call(mine, came, tiles):
    chunks = 2 * LATE
    return pl.pallas_call(
        functools.partial(late_kernel, mine),
        out_shape=[jax.ShapeDtypeStruct(a.shape, a.dtype) for a in tiles],
        in_specs=[ANY] * 9,
        out_specs=[ANY] * 7,
        input_output_aliases={2 + k: k for k in range(7)},
        scratch_shapes=[pltpu.VMEM((chunks, N, 8, LANES), F32), pltpu.VMEM((chunks, N, 8, LANES), BF16)] + dmas((chunks,), (chunks,)),
        compiler_params=params_of(),
        cost_estimate=pl.CostEstimate(flops=came[0].size * 1000, bytes_accessed=came[0].size * 12, transcendentals=0),
        name="late_chunks",
    )(*came, *tiles)


def local_step(*arrays):
    grads = arrays[:10]
    states = [a.reshape(LOCAL_ROWS, LANES) for a in arrays[10:13]]
    chunk = (N, 8, LANES)
    sds = jax.ShapeDtypeStruct
    vm = pltpu.VMEM
    deep = len(FRONT)
    late = (LATE * N, 8, LANES)
    two, three, eight, width = 2, 3, 8, 1152
    tile, tail, long = (eight, LANES), (56, LANES), (104, LANES)
    res = pl.pallas_call(
        step_kernel,
        out_shape=shapes(sds, F32, *[(LOCAL_ROWS, LANES)] * three) + shapes(sds, BF16, *[(c, eight, LANES) for c in COUNTS], (two, width), (two, width), (1, width))
        + shapes(sds, F32, (eight, LANES), (SEG_ROWS + TAIL, LANES), (two, SLOTS) + chunk, (2 * SLOTS + BOTH,) + chunk, (eight, SEG_TILES, eight, LANES), late, late),
        in_specs=[ANY] * 7 + [VMEM] * 3 + [ANY] * 3 + [SMEM],
        out_specs=[ANY] * 10 + [VMEM] * 4 + [ANY] * 6,
        scratch_shapes=shapes(vm, BF16, (three, two) + chunk)
        + shapes(vm, F32, (three, two) + chunk, (RING,) + chunk, (two, two) + chunk, (RING, two) + chunk, (two, three) + chunk, (two, ROWS, LANES),
                 (three, *tile), (three, *tile), (eight, LANES))
        + shapes(vm, BF16, (deep, 24, eight, LANES))
        + shapes(vm, F32, (eight, 192, LANES), (deep, TAIL, LANES), (TAIL, LANES), (three, *tail), (three, *long), long, tail, tail,
                 (ROWS + TAIL, LANES), (three, ROWS, LANES), (ROWS + TAIL, LANES), (5,) + chunk)
        + shapes(vm, BF16, (6,) + chunk)
        + dmas((RING, two), (three, two), (two, SLOTS), (2 * SLOTS + BOTH,), (three, two), (two, two), (two, three), (two,), (three,), (three,),
               (deep,), (deep,), (deep,), (6,), None, None, None, (three,), (deep,), None,
               (three, RING), (two, SLOTS), (BOTH,), (two, SLOTS), (two, HALF), (two, two), (4,), (three,), (5,), (6,)),
        compiler_params=params_of(collective_id=0),
        name="adamw_step",
    )(*[to_tiles(x) for x in grads[:7]], *grads[7:], *states, arrays[13].reshape(1))
    kept, (norm, spare_x, spare_y) = res[:10], (res[13], res[18], res[19])

    def swap(x, bit):
        return lax.ppermute(x, "dp", [(i, i ^ bit) for i in range(8)])
    came = (swap(spare_x, 4), swap(spare_y, 2))
    copied = list(copy_call(kept))
    *came, copied[4] = lax.optimization_barrier((*came, copied[4]))
    tiles = late_call(True, came, copied[3:])
    tiles = late_call(False, [swap(c, 1) for c in came], tiles)
    params = [from_tiles(t, x.shape[1:]) for t, x in zip(tiles, grads[:7])]
    return tuple([a.reshape(-1) for a in copied[:3]] + params + [res[10], res[11], res[12].reshape(-1), norm[0, 0]])


def solution(mesh):
    return jax.shard_map(local_step, mesh=mesh, in_specs=(P("dp"),) * 13 + (P(),), out_specs=(P("dp"),) * 3 + (P(),) * 11, check_vma=False)
```

time: 2260 us -> 975 us (0.43)
  waiting for transfers between devices: 1740 us -> 2.48 us
  Pallas kernels: 0 us -> 962 us
  local copies, waits for them, and re-layouts: 413 us -> 2.39 us
  other arithmetic: 57.3 us -> 0.62 us
  blocking collectives: 23.2 us -> 0 us
    unnamed x3 -> x0, waiting for transfers between devices: 1250 us -> none
    pallas_call x0 -> x4, Pallas kernels: none -> 962 us  [the longest x1 889 us: local_step(): pl.pallas_call(step_kernel, out_shape=shapes(sds, F32, *[(LOCAL_ROWS, LAN...]
    all_gather x1 -> x0, waiting for transfers between devices: 495 us -> none  [local_step(): full_master = lax.all_gather(new_master, 'dp', tiled=True)]
    unnamed x33 -> x8, local copies, waits for them, and re-layouts: 162 us -> 1.2 us
    reshape x7 -> x0, local copies, waits for them, and re-layouts: 95.9 us -> none  [split_flat(): tensors.append(flat_vec[offset:offset + piece_size].reshape(piece_shape))]
    slice x8 -> x1, local copies, waits for them, and re-layouts: 97.1 us -> 1.19 us  [local_step(): norm[0, 0]]
    convert_element_type x7 -> x0, local copies, waits for them, and re-layouts: 56.5 us -> none  [local_step(): local_grad.reshape(-1).astype(jnp.float32)]
    sub x1 -> x0, other arithmetic: 33.1 us -> none  [adam_update(): new_master = master - learn_rate * (decay_term + adam_dir)]
  transfers between devices with their start and end apart: 2 -> 4, of which waited for: 2 -> 1; matrix products, arithmetic and copies ran while one was open for 0% -> 0% of each run, Pallas kernels for 0% -> 7%
where the time goes in v3:
time: 975 us; the launch traced here: 972 us
  Pallas kernels  962 us (99%)
    pallas_call x1, Pallas kernels, local_step(): pl.pallas_call(step_kernel, out_shape=shapes(sds, F32, *[(LOCAL_ROWS, LAN...  889 us
    pallas_call x1, Pallas kernels, copy_call(): pl.pallas_call(copy_kernel, out_shape=[jax.ShapeDtypeStruct(a.shape, a.dt...  65.1 us
  transfers between devices with their start and end apart: 4, of which 1 were waited for; matrix products, arithmetic and copies ran while one was open for 0% of the time, Pallas kernels for 7%

profile of v3, /device:TPU:0, one launch (start us, length us, event | category | flops | bytes accessed | tf_op | source)
XLA Modules:
  0.0 972.1 jit_solution(13263346698092325812)
XLA Ops:
  1.3 889.4 %adamw_step.1 = (f32[27654,128]{1,0:T(8,128)}, f32[27654,128]{1,0:T(8,128)}, f32[27654,128]{1,0:T(8,128)}, bf16[2592,8,128]{2,1,0:T(8,128)(2,1)}, bf16[864,8,128...) custom-call(bf16[2592,8,128]{2,1,0:T(8,128)(2,1)} %bitcast.92, ...), custom_call_target="tpu_custom_call" | custom-call | tf_op jit(solution)/shard_map/adamw_step/pallas_call | solution.py:679
  890.7 2.4 collective-permute-start
  893.0 0.0 collective-permute-start.1
  893.0 0.0 copy-start.2
  893.0 65.1 %copy_results.1 = (f32[27654,128]{1,0:T(8,128)}, f32[27654,128]{1,0:T(8,128)}, f32[27654,128]{1,0:T(8,128)}, bf16[2592,8,128]{2,1,0:T(8,128)(2,1)}, bf16[864,8,1...) custom-call(f32[27654,128]{1,0:T(8,128)} %get-tuple-element.57.args_, ...), custom_call_target="tpu_custom_call" | custom-call | flops 19819929600 | bytes 198199296 | tf_op jit(solution)/shard_map/copy_results/pallas_call | solution.py:642
  958.1 0.0 collective-permute-done.args_0_
  958.2 0.0 collective-permute-done.1.args_1_
  958.2 0.4 collective-permute-start.2
  958.6 0.1 collective-permute-start.3
  958.7 1.2 slice.3
  959.9 0.0 copy-done.2
  959.9 0.6 reduce
  960.5 3.9 late_chunks.2
  964.5 0.0 collective-permute-done.2.args_0_
  964.5 2.5 collective-permute-done.3.args_1_
  966.9 0.0 copy-start.1
  967.0 0.0 copy-start
  967.0 4.0 late_chunks.3
  970.9 0.0 copy-done.1
  970.9 0.6 copy.59
  971.5 0.0 copy-done
  971.5 0.6 copy.60
Async XLA Ops:
  890.7 67.5 %collective-permute-start = (f32[648,8,128]{2,1,0:T(8,128)}, f32[648,8,128]{2,1,0:T(8,128)}, u32[]{:S(2)}, u32[]{:S(2)}) collective-permute-start(f32[648,8,128]{2,1,0:T(8,128)} %get-tuple-element.70), channel_id=1, source_target_pairs={{0,4},{1,5},{2,6},{3,7},{4,0},{5,1},{6,2},{7,3}} | collective-permute-start | bytes 7962632 | tf_op jit(solution)/shard_map/ppermute | solution.py:701
  893.0 65.1 %collective-permute-start.1 = (f32[648,8,128]{2,1,0:T(8,128)}, f32[648,8,128]{2,1,0:T(8,128)}, u32[]{:S(2)}, u32[]{:S(2)}) collective-permute-start(f32[648,8,128]{2,1,0:T(8,128)} %get-tuple-element.71), channel_id=1, source_target_pairs={{0,2},{1,3},{2,0},{3,1},{4,6},{5,7},{6,4},{7,5}} | collective-permute-start | bytes 7962632 | tf_op jit(solution)/shard_map/ppermute | solution.py:701
  893.0 66.9 %copy-start.2 = (bf16[1,1152]{1,0:T(2,128)(2,1)S(1)}, bf16[1,1152]{1,0:T(2,128)(2,1)}, u32[]{:S(2)}) copy-start(bf16[1,1152]{1,0:T(2,128)(2,1)} %get-tuple-element.98) | copy-start | bytes 6916
  958.2 6.3 collective-permute-start.2
  958.6 8.4 collective-permute-start.3
  966.9 4.0 copy-start.1
  967.0 4.6 copy-start

commit v4 on v3

--- a/solution.py
+++ b/solution.py
@@ -26,12 +26,12 @@
 MATRIX_ROWS = 8 * SEG_ROWS
 TAIL = 48
 WIN = 27600
-N = 216
+N = 144
 ROWS = N * 8
 HALF = SEG_TILES // 2 // N
 BOTH = 2 * HALF
 SLOTS = 3 * HALF
-LATE = 3
+LATE = 5
 RING = 4
 LAG = 5
 COUNTS = (2592, 864, 864, 2592, 6912, 6912, 6912)
@@ -132,7 +132,6 @@
     window_g[...] = jnp.zeros_like(window_g)
     halo[:, pl.ds(56, TAIL), :] = jnp.zeros((3, TAIL, LANES), F32)
     front[7] = jnp.zeros(front.shape[1:], F32)
-    greet(others)
 
     def raw_wait(kind, a):
         local(refs[0].at[pl.ds(0, N)], raw.at[kind, a], l_raw.at[kind, a]).wait()
@@ -205,9 +204,13 @@
     def own_jobs(j):
         return [(me, (h * HALF + j) * N, 2 * SLOTS + h * HALF + j) for h in pair]
 
-    def give(jobs, kind, par, wait_old):
+    def raw_loads(jobs, kind, turn):
         for a, (seg, tile, slot) in enumerate(jobs):
-            load_piece(refs, seg + flip, tile, raw.at[kind, a], l_raw.at[kind, a])
+            load_piece(refs, seg + turn, tile, raw.at[kind, a], l_raw.at[kind, a])
+
+    def give(jobs, kind, par, wait_old, load=True):
+        if load:
+            raw_loads(jobs, kind, flip)
         for a, (seg, tile, slot) in enumerate(jobs):
             raw_wait(kind, a)
             copy = to_partner(par, a, slot)
@@ -229,8 +232,7 @@
         @pl.when(s < SLOTS)
         def _():
             jobs = link_jobs(s)
-            for a, (seg, tile, slot) in enumerate(jobs):
-                load_piece(refs, seg, tile, raw.at[1, a], l_raw.at[1, a])
+            pl.when(s >= 1)(lambda: raw_loads(jobs, 1, 0))
             for a, (seg, tile, slot) in enumerate(jobs):
                 to_partner(0, a, slot).wait_recv()
                 local(land_p.at[slot], aux.at[0, a], l_aux.at[0, a]).start()
@@ -314,19 +316,28 @@
         row = pl.multiple_of(s * ROWS, 8)
         return local(g_flat.at[pl.ds(row, ROWS + TAIL)], gb, l_in.at[3])
 
-    give(link_jobs(0), 0, 0, False)
+    raw_loads(link_jobs(0), 0, flip)
+    raw_loads(link_jobs(0), 1, 0)
+    greet(others)
+    give(link_jobs(0), 0, 0, False, False)
     lax.fori_loop(0, SLOTS + LAG, step, 0)
     state_loads(0)
 
-    for r, dev in enumerate((partner, xn, yn)):
-        norm_send[r] = n_out[...]
-        copy = remote(norm_send.at[r], norm_land.at[r], s_n.at[r], r_n.at[r], dev)
-        copy.start()
-        copy.wait()
-        n_out[...] += norm_land[r]
+    gradient_load(0).start()
+
+    norm_send[...] = n_out[...]
+    norm_land[me] = n_out[...]
+
+    def norm_copy(o, dev, slot):
+        return remote(norm_send, norm_land.at[slot], s_n.at[o], r_n.at[slot], dev)
+    for o, dev in enumerate(others):
+        norm_copy(o, dev, me).start()
     for h in pair:
         local(own_g.at[h], g_flat.at[pl.ds(0, ROWS)], l_g.at[h]).wait()
-    gradient_load(0).start()
+    for o, dev in enumerate(others):
+        norm_copy(o, dev, me).wait_send()
+        norm_copy(o, dev, dev).wait_recv()
+    n_out[...] = jnp.sum(norm_land[...], axis=0)
     norm = jnp.sqrt(jnp.sum(n_out[...], axis=(0, 1), keepdims=True))
     o_norm[...] = jnp.broadcast_to(norm, (8, LANES))
     n_out[...] = jnp.broadcast_to(jnp.minimum(1.0, MAX_NORM / (norm + CLIP_EPS)), (8, LANES))
@@ -684,12 +695,12 @@
         out_specs=[ANY] * 10 + [VMEM] * 4 + [ANY] * 6,
         scratch_shapes=shapes(vm, BF16, (three, two) + chunk)
         + shapes(vm, F32, (three, two) + chunk, (RING,) + chunk, (two, two) + chunk, (RING, two) + chunk, (two, three) + chunk, (two, ROWS, LANES),
-                 (three, *tile), (three, *tile), (eight, LANES))
+                 tile, (eight, *tile), tile)
         + shapes(vm, BF16, (deep, 24, eight, LANES))
         + shapes(vm, F32, (eight, 192, LANES), (deep, TAIL, LANES), (TAIL, LANES), (three, *tail), (three, *long), long, tail, tail,
                  (ROWS + TAIL, LANES), (three, ROWS, LANES), (ROWS + TAIL, LANES), (5,) + chunk)
         + shapes(vm, BF16, (6,) + chunk)
-        + dmas((RING, two), (three, two), (two, SLOTS), (2 * SLOTS + BOTH,), (three, two), (two, two), (two, three), (two,), (three,), (three,),
+        + dmas((RING, two), (three, two), (two, SLOTS), (2 * SLOTS + BOTH,), (three, two), (two, two), (two, three), (two,), (deep,), (eight,),
                (deep,), (deep,), (deep,), (6,), None, None, None, (three,), (deep,), None,
                (three, RING), (two, SLOTS), (BOTH,), (two, SLOTS), (two, HALF), (two, two), (4,), (three,), (5,), (6,)),
         compiler_params=params_of(collective_id=0),

time: 975 us -> 967 us (level)
  Pallas kernels: 962 us -> 952 us
    pallas_call x1, Pallas kernels: 889 us -> 878 us  [local_step(): pl.pallas_call(step_kernel, out_shape=shapes(sds, F32, *[(LOCAL_ROWS, LAN...]
  transfers between devices with their start and end apart: 4 -> 4, of which waited for: 1 -> 2; matrix products, arithmetic and copies ran while one was open for 0% -> 0% of each run, Pallas kernels for 7% -> 7%
where the time goes in v4:
time: 967 us; the launch traced here: 962 us
  Pallas kernels  952 us (98%)
    pallas_call x1, Pallas kernels, local_step(): pl.pallas_call(step_kernel, out_shape=shapes(sds, F32, *[(LOCAL_ROWS, LAN...  878 us
    pallas_call x1, Pallas kernels, copy_call(): pl.pallas_call(copy_kernel, out_shape=[jax.ShapeDtypeStruct(a.shape, a.dt...  65.1 us
  transfers between devices with their start and end apart: 4, of which 2 were waited for; matrix products, arithmetic and copies ran while one was open for 0% of the time, Pallas kernels for 7%

profile of v4, /device:TPU:0, one launch (start us, length us, event | category | flops | bytes accessed | tf_op | source)
XLA Modules:
  0.0 962.2 jit_solution(1871047470817427148)
XLA Ops:
  1.3 878.3 %adamw_step.1 = (f32[27654,128]{1,0:T(8,128)}, f32[27654,128]{1,0:T(8,128)}, f32[27654,128]{1,0:T(8,128)}, bf16[2592,8,128]{2,1,0:T(8,128)(2,1)}, bf16[864,8,128...) custom-call(bf16[2592,8,128]{2,1,0:T(8,128)(2,1)} %bitcast.92, ...), custom_call_target="tpu_custom_call" | custom-call | tf_op jit(solution)/shard_map/adamw_step/pallas_call | solution.py:690
  879.6 1.7 collective-permute-start
  881.3 0.2 collective-permute-start.1
  881.5 0.0 copy-start.2
  881.5 65.1 %copy_results.1 = (f32[27654,128]{1,0:T(8,128)}, f32[27654,128]{1,0:T(8,128)}, f32[27654,128]{1,0:T(8,128)}, bf16[2592,8,128]{2,1,0:T(8,128)(2,1)}, bf16[864,8,1...) custom-call(f32[27654,128]{1,0:T(8,128)} %get-tuple-element.57.args_, ...), custom_call_target="tpu_custom_call" | custom-call | flops 19819929600 | bytes 198199296 | tf_op jit(solution)/shard_map/copy_results/pallas_call | solution.py:653
  946.6 0.0 collective-permute-done.args_0_
  946.6 0.5 collective-permute-done.1.args_1_
  947.1 0.0 collective-permute-start.2
  947.1 0.5 collective-permute-start.3
  947.6 1.2 slice.3
  948.8 0.0 copy-done.2
  948.8 0.6 reduce
  949.4 4.3 late_chunks.2
  953.7 0.0 collective-permute-done.2.args_0_
  953.7 2.9 collective-permute-done.3.args_1_
  956.6 0.0 copy-start.1
  956.6 0.0 copy-start
  956.6 4.3 late_chunks.3
  961.0 0.0 copy-done.1
  961.0 0.6 copy.59
  961.6 0.0 copy-done
  961.6 0.6 copy.60
Async XLA Ops:
  879.6 67.0 %collective-permute-start = (f32[720,8,128]{2,1,0:T(8,128)}, f32[720,8,128]{2,1,0:T(8,128)}, u32[]{:S(2)}, u32[]{:S(2)}) collective-permute-start(f32[720,8,128]{2,1,0:T(8,128)} %get-tuple-element.70), channel_id=1, source_target_pairs={{0,4},{1,5},{2,6},{3,7},{4,0},{5,1},{6,2},{7,3}} | collective-permute-start | bytes 8847368 | tf_op jit(solution)/shard_map/ppermute | solution.py:712
  881.3 65.7 %collective-permute-start.1 = (f32[720,8,128]{2,1,0:T(8,128)}, f32[720,8,128]{2,1,0:T(8,128)}, u32[]{:S(2)}, u32[]{:S(2)}) collective-permute-start(f32[720,8,128]{2,1,0:T(8,128)} %get-tuple-element.71), channel_id=1, source_target_pairs={{0,2},{1,3},{2,0},{3,1},{4,6},{5,7},{6,4},{7,5}} | collective-permute-start | bytes 8847368 | tf_op jit(solution)/shard_map/ppermute | solution.py:712
  881.5 67.3 %copy-start.2 = (bf16[1,1152]{1,0:T(2,128)(2,1)S(1)}, bf16[1,1152]{1,0:T(2,128)(2,1)}, u32[]{:S(2)}) copy-start(bf16[1,1152]{1,0:T(2,128)(2,1)} %get-tuple-element.98) | copy-start | bytes 6916
  947.1 6.6 collective-permute-start.2
  947.1 9.5 collective-permute-start.3
  956.6 4.3 copy-start.1
  956.6 5.0 copy-start

commit v5 on v4

--- a/solution.py
+++ b/solution.py
@@ -113,12 +113,12 @@
 def step_kernel(*args):
     refs, small, ins, rate = args[:7], args[7:10], args[10:13], args[13]
     outs, outs7, gains_out, o_norm = args[14:17], args[17:24], args[24:27], args[27]
-    g_flat, land_l, land_p, land, spare_x, spare_y = args[28:34]
+    g_flat, land_l, land_p, land, spare_x, spare_y, end_x, end_y = args[28:36]
     (raw, stage_p, stage_u, aux, stage, own_in, own_g, norm_send, norm_land, n_out, front_raw, front, front_land, tail_g,
-     window, halo, window_g, gains_send, gains_land, gb, st, pb, cin, cout) = args[34:58]
+     window, halo, window_g, gains_send, gains_land, gb, st, pb, cin, cout) = args[36:60]
     (s_l, s_p, r_l, r_p, l_raw, l_aux, l_own, l_g, s_n, r_n, l_front, s_front, r_front, l_win, s_win, r_win, l_tail, l_six, s_gain, r_gain,
-     su, ru, ru_o, r_d, s_f, s_d, l_in, l_out, l_c, l_so) = args[58:]
-    spare = (spare_x, spare_y)
+     su, ru, ru_o, r_d, s_f, s_d, l_in, l_out, l_c, l_so) = args[60:]
+    spare, ends = (spare_x, spare_y), (end_x, end_y)
     me = lax.axis_index("dp")
     flip, partner, xn, yn, diag = neighbours(me)
     links = (xn, yn)
@@ -308,21 +308,20 @@
             out.start()
 
     def state_loads(s):
-        row = pl.multiple_of(s * ROWS, 8)
-        for a in trio:
-            local(ins[a].at[pl.ds(row, ROWS)], st.at[a], l_in.at[a]).start()
+        row, par = pl.multiple_of(s * ROWS, 8), lax.rem(s, 2)
+        return [local(ins[a].at[pl.ds(row, ROWS)], st.at[par, a], l_in.at[par, a]) for a in trio]
 
     def gradient_load(s):
-        row = pl.multiple_of(s * ROWS, 8)
-        return local(g_flat.at[pl.ds(row, ROWS + TAIL)], gb, l_in.at[3])
+        row, par = pl.multiple_of(s * ROWS, 8), lax.rem(s, 2)
+        return local(g_flat.at[pl.ds(row, ROWS + TAIL)], gb.at[par], l_in.at[par, 3])
 
     raw_loads(link_jobs(0), 0, flip)
     raw_loads(link_jobs(0), 1, 0)
     greet(others)
     give(link_jobs(0), 0, 0, False, False)
     lax.fori_loop(0, SLOTS + LAG, step, 0)
-    state_loads(0)
-
+    for load in state_loads(0):
+        load.start()
     gradient_load(0).start()
 
     norm_send[...] = n_out[...]
@@ -395,7 +394,7 @@
 
     def first_rows():
         part = pl.ds(54 - shift, TAIL)
-        pb[pl.ds(0, TAIL), :] = adam(gb[pl.ds(0, TAIL), :] * coef, halo[0, part, :], halo[1, part, :], halo[2, part, :], lr, WEIGHT_DECAY)[0]
+        pb[pl.ds(0, TAIL), :] = adam(gb[0, pl.ds(0, TAIL), :] * coef, *[halo[a, part, :] for a in trio], lr, WEIGHT_DECAY)[0]
 
     def at(seg, c):
         return land.at[seg, pl.ds(pl.multiple_of(c * N, N), N)]
@@ -414,18 +413,19 @@
         ring = lax.rem(s, RING)
         row = pl.multiple_of(s * ROWS, 8)
 
-        def state_store(a):
-            return local(st.at[a], outs[a].at[pl.ds(row, ROWS)], l_out.at[a])
-
-        @pl.when(s >= 1)
-        def _():
-            gradient_load(s).start()
-            for a in trio:
-                state_store(a).wait()
-            state_loads(s)
-        gradient_load(s).wait()
-        for a in trio:
-            local(ins[a].at[pl.ds(row, ROWS)], st.at[a], l_in.at[a]).wait()
+        par = lax.rem(s, 2)
+
+        def state_store(a, par):
+            return local(st.at[par, a], outs[a].at[pl.ds(row, ROWS)], l_out.at[par, a])
+
+        @pl.when(s < BOTH - 1)
+        def _():
+            gradient_load(s + 1).start()
+            for a, load in enumerate(state_loads(s + 1)):
+                pl.when(s >= 1)(state_store(a, 1 - par).wait)
+                load.start()
+        for load in state_loads(s) + [gradient_load(s)]:
+            load.wait()
         pl.when(s == 0)(first_rows)
         slab = 48
         base = me * LOCAL_ROWS + s * ROWS
@@ -435,14 +435,14 @@
             e = pl.ds(i * slab + shift, slab)
             rows = lax.broadcasted_iota(jnp.int32, (slab, LANES), 0) + (base + i * slab)
             decay = jnp.where(rows < MATRIX_ROWS, WEIGHT_DECAY, 0.0)
-            new = adam(gb[e, :] * coef, st[0, d, :], st[1, d, :], st[2, d, :], lr, decay)
+            new = adam(gb[par, e, :] * coef, *[st[par, a, d, :] for a in trio], lr, decay)
             for a in trio:
-                st[a, d, :] = new[a]
+                st[par, a, d, :] = new[a]
             pb[e, :] = new[0]
             return carry
         lax.fori_loop(0, ROWS // slab, update, 0)
         for a in trio:
-            state_store(a).start()
+            state_store(a, par).start()
         devs = links + (partner,)
 
         @pl.when(s >= RING)
@@ -481,16 +481,21 @@
     def stored(k):
         local(cout.at[k], outs7[0].at[pl.ds(0, N)], l_so.at[k]).wait()
 
-    last = SLOTS - LATE
+    last = SLOTS - LATE - 1
+    spot = at(0, 0)
 
     def link_wait(a, q):
-        return remote(at(0, 0), at(0, 0), s_d.at[a, 0], ru.at[a, q], links[a])
+        return remote(spot, spot, s_d.at[a, 0], ru.at[a, q], links[a])
 
     def hand(a, par, q, src, dst):
         return remote(src, dst, s_d.at[a, par], r_d.at[a, q], partner)
 
-    def forward(a, seg, chunk, j):
-        return remote(at(seg, chunk), at(seg, chunk), s_f.at[a, j], ru.at[a, BOTH + j], links[a])
+    def forward(a, seg, chunk, j, dst):
+        return remote(at(seg, chunk), dst, s_f.at[a, j], ru.at[a, BOTH + j], links[a])
+
+    def start_forward(a, seg, chunk, j):
+        pl.when(j < HALF - LATE - 1)(lambda: forward(a, seg, chunk, j, at(seg, chunk)).start())
+        pl.when(j == HALF - LATE - 1)(lambda: forward(a, seg, chunk, j, ends[a]).start())
 
     def gather_step(s, carry):
         j = s - BOTH
@@ -506,8 +511,8 @@
 
         @pl.when((j >= 0) & (j < HALF - LATE))
         def _():
-            forward(1, xn, j, j).start()
-            forward(0, yn, HALF + j, j).start()
+            start_forward(1, xn, j, j)
+            start_forward(0, yn, HALF + j, j)
 
         @pl.when((q >= 1) & (q <= last))
         def _():
@@ -526,7 +531,7 @@
             for a in pair:
                 seg, chunk = link_piece(q, a)
                 link_wait(a, q).wait_recv()
-                pl.when(q >= 2)(hand(a, par, q, at(0, 0), at(0, 0)).wait_send)
+                pl.when(q >= 2)(hand(a, par, q, spot, spot).wait_send)
 
                 def act(ref, a=a, seg=seg, chunk=chunk):
                     hand(a, par, q, ref, at(seg, chunk)).start()
@@ -535,14 +540,14 @@
 
         @pl.when(own_partner)
         def _():
-            remote(at(0, 0), at(0, 0), su.at[2, 0], ru_o.at[z], partner).wait_recv()
+            remote(spot, spot, su.at[2, 0], ru_o.at[z], partner).wait_recv()
             fetch(4, at(partner, z))
 
         @pl.when(from_partner)
         def _():
             for a in pair:
                 seg, chunk = link_piece(z, a)
-                hand(a, 0, z, at(0, 0), at(0, 0)).wait_recv()
+                hand(a, 0, z, spot, spot).wait_recv()
                 fetch(2 + a, at(seg + flip, chunk))
 
         @pl.when(arrives)
@@ -562,13 +567,16 @@
     lax.fori_loop(0, last + LAG + 1, gather_step, 0)
     gains_finish()
     for a in pair:
+        link_wait(a, last).wait_recv()
+    for a in pair:
         stored(2 + a)
         for par in pair:
-            hand(a, par, 0, at(0, 0), at(0, 0)).wait_send()
+            hand(a, par, 0, spot, spot).wait_send()
         for j in range(HALF - LATE):
-            forward(a, 0, 0, j).wait_send()
+            forward(a, 0, 0, j, spot).wait_send()
     for a in trio:
-        local(st.at[a], outs[a].at[pl.ds(0, ROWS)], l_out.at[a]).wait()
+        for par in pair:
+            local(st.at[par, a], outs[a].at[pl.ds(0, ROWS)], l_out.at[par, a]).wait()
         for ring in range(RING):
             remote(stage_u.at[ring], at(me, 0), su.at[a, ring], ru_o.at[0], partner).wait_send()
 
@@ -599,12 +607,12 @@
 
 
 def late_kernel(mine, *args):
-    came, outs7 = args[:2], args[9:16]
-    cin, cout, l_in, l_out = args[16:]
+    came, ends, outs7 = args[:2], args[2:4], args[11:18]
+    cin, cout, l_in, l_out = args[18:]
     flip, partner, xn, yn, diag = neighbours(lax.axis_index("dp"))
     seg = diag if mine else diag + flip
-    jobs = [(a, i, a * LATE + i) for a in range(2) for i in range(LATE)]
-    loads = [local(came[a].at[pl.ds(i * N, N)], cin.at[k], l_in.at[k]) for a, i, k in jobs]
+    jobs = [(a, i, a * (LATE + 1) + i) for a in range(2) for i in range(LATE + 1)]
+    loads = [local(came[a].at[pl.ds(i * N, N)] if i < LATE else ends[a], cin.at[k], l_in.at[k]) for a, i, k in jobs]
     for load in loads:
         load.start()
     for a, i, k in jobs:
@@ -613,8 +621,9 @@
         def conv(d, k=k):
             cout[k, d] = cin[k, d].astype(BF16)
         tiles_loop(conv)
-        store_piece(outs7, seg, ((1 + a) * HALF - LATE + i) * N + 0 * seg, cout.at[k], l_out.at[k])
-    for k in range(2 * LATE):
+        chunk = (1 + a) * HALF - LATE + (i if i < LATE else -1)
+        store_piece(outs7, seg, chunk * N + 0 * seg, cout.at[k], l_out.at[k])
+    for a, i, k in jobs:
         local(cout.at[k], outs7[0].at[pl.ds(0, N)], l_out.at[k]).wait()
 
 
@@ -663,13 +672,13 @@
 
 
 def late_call(mine, came, tiles):
-    chunks = 2 * LATE
+    chunks = 2 * LATE + 2
     return pl.pallas_call(
         functools.partial(late_kernel, mine),
         out_shape=[jax.ShapeDtypeStruct(a.shape, a.dtype) for a in tiles],
-        in_specs=[ANY] * 9,
+        in_specs=[ANY] * 11,
         out_specs=[ANY] * 7,
-        input_output_aliases={2 + k: k for k in range(7)},
+        input_output_aliases={4 + k: k for k in range(7)},
         scratch_shapes=[pltpu.VMEM((chunks, N, 8, LANES), F32), pltpu.VMEM((chunks, N, 8, LANES), BF16)] + dmas((chunks,), (chunks,)),
         compiler_params=params_of(),
         cost_estimate=pl.CostEstimate(flops=came[0].size * 1000, bytes_accessed=came[0].size * 12, transcendentals=0),
@@ -690,31 +699,32 @@
     res = pl.pallas_call(
         step_kernel,
         out_shape=shapes(sds, F32, *[(LOCAL_ROWS, LANES)] * three) + shapes(sds, BF16, *[(c, eight, LANES) for c in COUNTS], (two, width), (two, width), (1, width))
-        + shapes(sds, F32, (eight, LANES), (SEG_ROWS + TAIL, LANES), (two, SLOTS) + chunk, (2 * SLOTS + BOTH,) + chunk, (eight, SEG_TILES, eight, LANES), late, late),
+        + shapes(sds, F32, (eight, LANES), (SEG_ROWS + TAIL, LANES), (two, SLOTS) + chunk, (2 * SLOTS + BOTH,) + chunk, (eight, SEG_TILES, eight, LANES), late, late, chunk, chunk),
         in_specs=[ANY] * 7 + [VMEM] * 3 + [ANY] * 3 + [SMEM],
-        out_specs=[ANY] * 10 + [VMEM] * 4 + [ANY] * 6,
+        out_specs=[ANY] * 10 + [VMEM] * 4 + [ANY] * 8,
         scratch_shapes=shapes(vm, BF16, (three, two) + chunk)
         + shapes(vm, F32, (three, two) + chunk, (RING,) + chunk, (two, two) + chunk, (RING, two) + chunk, (two, three) + chunk, (two, ROWS, LANES),
                  tile, (eight, *tile), tile)
         + shapes(vm, BF16, (deep, 24, eight, LANES))
         + shapes(vm, F32, (eight, 192, LANES), (deep, TAIL, LANES), (TAIL, LANES), (three, *tail), (three, *long), long, tail, tail,
-                 (ROWS + TAIL, LANES), (three, ROWS, LANES), (ROWS + TAIL, LANES), (5,) + chunk)
+                 (two, ROWS + TAIL, LANES), (two, three, ROWS, LANES), (ROWS + TAIL, LANES), (5,) + chunk)
         + shapes(vm, BF16, (6,) + chunk)
         + dmas((RING, two), (three, two), (two, SLOTS), (2 * SLOTS + BOTH,), (three, two), (two, two), (two, three), (two,), (deep,), (eight,),
                (deep,), (deep,), (deep,), (6,), None, None, None, (three,), (deep,), None,
-               (three, RING), (two, SLOTS), (BOTH,), (two, SLOTS), (two, HALF), (two, two), (4,), (three,), (5,), (6,)),
+               (three, RING), (two, SLOTS), (BOTH,), (two, SLOTS), (two, HALF), (two, two), (two, 4), (two, three), (5,), (6,)),
         compiler_params=params_of(collective_id=0),
         name="adamw_step",
     )(*[to_tiles(x) for x in grads[:7]], *grads[7:], *states, arrays[13].reshape(1))
-    kept, (norm, spare_x, spare_y) = res[:10], (res[13], res[18], res[19])
+    kept, (norm, spare_x, spare_y) = res[:10], (res[13], *res[18:20])
 
     def swap(x, bit):
         return lax.ppermute(x, "dp", [(i, i ^ bit) for i in range(8)])
-    came = (swap(spare_x, 4), swap(spare_y, 2))
+    ends = res[:-3:-1]
+    came = [swap(spare_x, 4), swap(spare_y, 2)] + [swap(e, 1) for e in ends]
     copied = list(copy_call(kept))
     *came, copied[4] = lax.optimization_barrier((*came, copied[4]))
-    tiles = late_call(True, came, copied[3:])
-    tiles = late_call(False, [swap(c, 1) for c in came], tiles)
+    tiles = late_call(True, (*came[:2], *ends), copied[3:])
+    tiles = late_call(False, (*[swap(c, 1) for c in came[:2]], *came[2:]), tiles)
     params = [from_tiles(t, x.shape[1:]) for t, x in zip(tiles, grads[:7])]
     return tuple([a.reshape(-1) for a in copied[:3]] + params + [res[10], res[11], res[12].reshape(-1), norm[0, 0]])
 

time: 967 us -> 963 us (level)
  transfers between devices with their start and end apart: 4 -> 6, of which waited for: 2 -> 1; matrix products, arithmetic and copies ran while one was open for 0% -> 0% of each run, Pallas kernels for 7% -> 7%
where the time goes in v5:
time: 963 us; the launch traced here: 959 us
  Pallas kernels  949 us (99%)
    pallas_call x1, Pallas kernels, local_step(): pl.pallas_call(step_kernel, out_shape=shapes(sds, F32, *[(LOCAL_ROWS, LAN...  874 us
    pallas_call x1, Pallas kernels, copy_call(): pl.pallas_call(copy_kernel, out_shape=[jax.ShapeDtypeStruct(a.shape, a.dt...  65.1 us
  transfers between devices with their start and end apart: 6, of which 1 were waited for; matrix products, arithmetic and copies ran while one was open for 0% of the time, Pallas kernels for 7%

profile of v5, /device:TPU:0, one launch (start us, length us, event | category | flops | bytes accessed | tf_op | source)
XLA Modules:
  0.0 958.7 jit_solution(12466108606608908313)
XLA Ops:
  1.3 874.0 %adamw_step.1 = (f32[27654,128]{1,0:T(8,128)}, f32[27654,128]{1,0:T(8,128)}, f32[27654,128]{1,0:T(8,128)}, bf16[2592,8,128]{2,1,0:T(8,128)(2,1)}, bf16[864,8,128...) custom-call(bf16[2592,8,128]{2,1,0:T(8,128)(2,1)} %bitcast.92, ...), custom_call_target="tpu_custom_call" | custom-call | tf_op jit(solution)/shard_map/adamw_step/pallas_call | solution.py:699
  875.3 1.5 collective-permute-start
  876.8 0.5 collective-permute-start.1
  877.3 0.0 collective-permute-start.2
  877.3 0.5 collective-permute-start.3
  877.8 0.0 copy-start.4
  877.8 65.1 %copy_results.1 = (f32[27654,128]{1,0:T(8,128)}, f32[27654,128]{1,0:T(8,128)}, f32[27654,128]{1,0:T(8,128)}, bf16[2592,8,128]{2,1,0:T(8,128)(2,1)}, bf16[864,8,1...) custom-call(f32[27654,128]{1,0:T(8,128)} %get-tuple-element.61.args_, ...), custom_call_target="tpu_custom_call" | custom-call | flops 19819929600 | bytes 198199296 | tf_op jit(solution)/shard_map/copy_results/pallas_call | solution.py:662
  943.0 0.0 collective-permute-done.2.args_2_
  943.0 0.0 copy-start
  943.0 0.0 collective-permute-done.3.args_3_
  943.0 0.0 copy-start.1
  943.0 0.0 collective-permute-done.args_0_
  943.0 0.0 collective-permute-done.1.args_1_
  943.0 0.0 collective-permute-start.4
  943.1 0.5 collective-permute-start.5
  943.5 1.2 slice.3
  944.7 0.0 copy-done.4
  944.7 0.6 reduce
  945.4 4.8 late_chunks.2
  950.2 0.0 copy-done
  950.2 0.0 copy-done.1
  950.2 0.0 collective-permute-done.4.args_0_
  950.2 2.3 collective-permute-done.5.args_1_
  952.6 0.0 copy-start.3
  952.6 0.0 copy-start.2
  952.6 4.9 late_chunks.3
  957.5 0.0 copy-done.3
  957.5 0.6 copy.59
  958.1 0.0 copy-done.2
  958.1 0.6 copy.60
Async XLA Ops:
  875.3 67.7 %collective-permute-start = (f32[720,8,128]{2,1,0:T(8,128)}, f32[720,8,128]{2,1,0:T(8,128)}, u32[]{:S(2)}, u32[]{:S(2)}) collective-permute-start(f32[720,8,128]{2,1,0:T(8,128)} %get-tuple-element.74), channel_id=1, source_target_pairs={{0,4},{1,5},{2,6},{3,7},{4,0},{5,1},{6,2},{7,3}} | collective-permute-start | bytes 8847368 | tf_op jit(solution)/shard_map/ppermute | solution.py:721
  876.8 66.2 %collective-permute-start.1 = (f32[720,8,128]{2,1,0:T(8,128)}, f32[720,8,128]{2,1,0:T(8,128)}, u32[]{:S(2)}, u32[]{:S(2)}) collective-permute-start(f32[720,8,128]{2,1,0:T(8,128)} %get-tuple-element.75), channel_id=1, source_target_pairs={{0,2},{1,3},{2,0},{3,1},{4,6},{5,7},{6,4},{7,5}} | collective-permute-start | bytes 8847368 | tf_op jit(solution)/shard_map/ppermute | solution.py:721
  877.3 65.6 %collective-permute-start.2 = (f32[144,8,128]{2,1,0:T(8,128)}, f32[144,8,128]{2,1,0:T(8,128)S(1)}, u32[]{:S(2)}, u32[]{:S(2)}) collective-permute-start(f32[144,8,128]{2,1,0:T(8,128)} %get-tuple-element.76.args_2_), channel_id=1, source_target_pairs={{0,1},{1,0},{2,3},{3,2},{4,5},{5,4},{6,7},{7,6}} | collective-permute-start | bytes 1769480 | tf_op jit(solution)/shard_map/ppermute | solution.py:721
  877.3 65.6 %collective-permute-start.3 = (f32[144,8,128]{2,1,0:T(8,128)}, f32[144,8,128]{2,1,0:T(8,128)S(1)}, u32[]{:S(2)}, u32[]{:S(2)}) collective-permute-start(f32[144,8,128]{2,1,0:T(8,128)} %get-tuple-element.77.args_3_), channel_id=1, source_target_pairs={{0,1},{1,0},{2,3},{3,2},{4,5},{5,4},{6,7},{7,6}} | collective-permute-start | bytes 1769480 | tf_op jit(solution)/shard_map/ppermute | solution.py:721
  877.8 66.9 %copy-start.4 = (bf16[1,1152]{1,0:T(2,128)(2,1)S(1)}, bf16[1,1152]{1,0:T(2,128)(2,1)}, u32[]{:S(2)}) copy-start(bf16[1,1152]{1,0:T(2,128)(2,1)} %get-tuple-element.106) | copy-start | bytes 6916
  943.0 7.2 copy-start
  943.0 7.2 copy-start.1
  943.0 7.2 collective-permute-start.4
  943.1 9.5 collective-permute-start.5
  952.6 4.9 copy-start.3
  952.6 5.5 copy-start.2

commit v6 on v5

--- a/solution.py
+++ b/solution.py
@@ -227,12 +227,12 @@
 
         @pl.when(s < SLOTS - 1)
         def _():
-            give(link_jobs(s + 1), 0, lax.rem(s + 1, 2), s >= 1)
+            give(link_jobs(s + 1), 0, lax.rem(s + 1, 2), s >= 1, False)
+            pl.when(s < SLOTS - 2)(lambda: raw_loads(link_jobs(s + 2), 0, flip))
 
         @pl.when(s < SLOTS)
         def _():
             jobs = link_jobs(s)
-            pl.when(s >= 1)(lambda: raw_loads(jobs, 1, 0))
             for a, (seg, tile, slot) in enumerate(jobs):
                 to_partner(0, a, slot).wait_recv()
                 local(land_p.at[slot], aux.at[0, a], l_aux.at[0, a]).start()
@@ -263,13 +263,14 @@
                         stage[ring, a, d] = raw[1, a, d].astype(F32) + aux[0, a, d] + aux[1, a, d]
                     tiles_loop(add)
                 copy.start()
+            pl.when(s < SLOTS - 1)(lambda: raw_loads(link_jobs(s + 1), 1, 0))
 
         pl.when(s == 2)(small_exchange)
-        pl.when(s == BOTH + 4)(small_finish)
-
-        @pl.when((s >= HALF + 4) & (s < BOTH + 4))
-        def _():
-            give(own_jobs(s - HALF - 4), 2, 2, s > HALF + 4)
+        pl.when(s == BOTH + RING)(small_finish)
+
+        @pl.when((s >= HALF + RING) & (s < BOTH + RING))
+        def _():
+            give(own_jobs(s - HALF - RING), 2, 2, s > HALF + RING)
 
         @pl.when(s >= BOTH + LAG)
         def _():
@@ -319,6 +320,7 @@
     raw_loads(link_jobs(0), 1, 0)
     greet(others)
     give(link_jobs(0), 0, 0, False, False)
+    raw_loads(link_jobs(1), 0, flip)
     lax.fori_loop(0, SLOTS + LAG, step, 0)
     for load in state_loads(0):
         load.start()

time: 963 us -> 962 us (level)
  no operation moved by 1% of the time
where the time goes in v6:
time: 962 us; the launch traced here: 959 us
  Pallas kernels  949 us (99%)
    pallas_call x1, Pallas kernels, local_step(): pl.pallas_call(step_kernel, out_shape=shapes(sds, F32, *[(LOCAL_ROWS, LAN...  874 us
    pallas_call x1, Pallas kernels, copy_call(): pl.pallas_call(copy_kernel, out_shape=[jax.ShapeDtypeStruct(a.shape, a.dt...  65.1 us
  transfers between devices with their start and end apart: 6, of which 1 were waited for; matrix products, arithmetic and copies ran while one was open for 0% of the time, Pallas kernels for 7%

profile of v6, /device:TPU:0, one launch (start us, length us, event | category | flops | bytes accessed | tf_op | source)
XLA Modules:
  0.0 958.6 jit_solution(11728537496553344089)
XLA Ops:
  1.3 874.0 %adamw_step.1 = (f32[27654,128]{1,0:T(8,128)}, f32[27654,128]{1,0:T(8,128)}, f32[27654,128]{1,0:T(8,128)}, bf16[2592,8,128]{2,1,0:T(8,128)(2,1)}, bf16[864,8,128...) custom-call(bf16[2592,8,128]{2,1,0:T(8,128)(2,1)} %bitcast.92, ...), custom_call_target="tpu_custom_call" | custom-call | tf_op jit(solution)/shard_map/adamw_step/pallas_call | solution.py:701
  875.3 1.5 collective-permute-start
  876.8 0.5 collective-permute-start.1
  877.3 0.0 collective-permute-start.2
  877.3 0.5 collective-permute-start.3
  877.8 0.0 copy-start.4
  877.8 65.1 %copy_results.1 = (f32[27654,128]{1,0:T(8,128)}, f32[27654,128]{1,0:T(8,128)}, f32[27654,128]{1,0:T(8,128)}, bf16[2592,8,128]{2,1,0:T(8,128)(2,1)}, bf16[864,8,1...) custom-call(f32[27654,128]{1,0:T(8,128)} %get-tuple-element.61.args_, ...), custom_call_target="tpu_custom_call" | custom-call | flops 19819929600 | bytes 198199296 | tf_op jit(solution)/shard_map/copy_results/pallas_call | solution.py:664
  942.9 0.0 collective-permute-done.2.args_2_
  943.0 0.0 copy-start
  943.0 0.0 collective-permute-done.3.args_3_
  943.0 0.0 copy-start.1
  943.0 0.0 collective-permute-done.args_0_
  943.0 0.0 collective-permute-done.1.args_1_
  943.0 0.0 collective-permute-start.4
  943.0 0.5 collective-permute-start.5
  943.5 1.2 slice.3
  944.7 0.0 copy-done.4
  944.7 0.6 reduce
  945.3 4.8 late_chunks.2
  950.2 0.0 copy-done
  950.2 0.0 copy-done.1
  950.2 0.0 collective-permute-done.4.args_0_
  950.2 2.3 collective-permute-done.5.args_1_
  952.6 0.0 copy-start.3
  952.6 0.0 copy-start.2
  952.6 4.9 late_chunks.3
  957.4 0.0 copy-done.3
  957.5 0.6 copy.59
  958.1 0.0 copy-done.2
  958.1 0.6 copy.60
Async XLA Ops:
  875.3 67.7 %collective-permute-start = (f32[720,8,128]{2,1,0:T(8,128)}, f32[720,8,128]{2,1,0:T(8,128)}, u32[]{:S(2)}, u32[]{:S(2)}) collective-permute-start(f32[720,8,128]{2,1,0:T(8,128)} %get-tuple-element.74), channel_id=1, source_target_pairs={{0,4},{1,5},{2,6},{3,7},{4,0},{5,1},{6,2},{7,3}} | collective-permute-start | bytes 8847368 | tf_op jit(solution)/shard_map/ppermute | solution.py:723
  876.8 66.2 %collective-permute-start.1 = (f32[720,8,128]{2,1,0:T(8,128)}, f32[720,8,128]{2,1,0:T(8,128)}, u32[]{:S(2)}, u32[]{:S(2)}) collective-permute-start(f32[720,8,128]{2,1,0:T(8,128)} %get-tuple-element.75), channel_id=1, source_target_pairs={{0,2},{1,3},{2,0},{3,1},{4,6},{5,7},{6,4},{7,5}} | collective-permute-start | bytes 8847368 | tf_op jit(solution)/shard_map/ppermute | solution.py:723
  877.3 65.6 %collective-permute-start.2 = (f32[144,8,128]{2,1,0:T(8,128)}, f32[144,8,128]{2,1,0:T(8,128)S(1)}, u32[]{:S(2)}, u32[]{:S(2)}) collective-permute-start(f32[144,8,128]{2,1,0:T(8,128)} %get-tuple-element.76.args_2_), channel_id=1, source_target_pairs={{0,1},{1,0},{2,3},{3,2},{4,5},{5,4},{6,7},{7,6}} | collective-permute-start | bytes 1769480 | tf_op jit(solution)/shard_map/ppermute | solution.py:723
  877.3 65.6 %collective-permute-start.3 = (f32[144,8,128]{2,1,0:T(8,128)}, f32[144,8,128]{2,1,0:T(8,128)S(1)}, u32[]{:S(2)}, u32[]{:S(2)}) collective-permute-start(f32[144,8,128]{2,1,0:T(8,128)} %get-tuple-element.77.args_3_), channel_id=1, source_target_pairs={{0,1},{1,0},{2,3},{3,2},{4,5},{5,4},{6,7},{7,6}} | collective-permute-start | bytes 1769480 | tf_op jit(solution)/shard_map/ppermute | solution.py:723
  877.8 66.9 %copy-start.4 = (bf16[1,1152]{1,0:T(2,128)(2,1)S(1)}, bf16[1,1152]{1,0:T(2,128)(2,1)}, u32[]{:S(2)}) copy-start(bf16[1,1152]{1,0:T(2,128)(2,1)} %get-tuple-element.106) | copy-start | bytes 6916
  943.0 7.2 copy-start
  943.0 7.2 copy-start.1
  943.0 7.2 collective-permute-start.4
  943.0 9.5 collective-permute-start.5
  952.6 4.9 copy-start.3
  952.6 5.5 copy-start.2
